TPU v7x, 32 devices: a whole 2x2x4 slice. The times are simulated.
32 devices in a mesh: mem: 2 (over x), col: 16 (over z, y, core).
Axes of the slice: x: 2, y: 2, z: 4, core: 2. Of those that a mesh axis runs over, the one named last changes fastest.
Arguments:
- state_a: bfloat16 [64, 1048576], P('mem', 'col'), may hold values from -12 to 12
- state_b: bfloat16 [64, 1048576], P('mem', 'col'), may hold values from -12 to 12
- obs_index: int32 [2, 8192, 16], P(None, ('col', 'mem')), may hold values from 0 to 127
- observation_count: int32 [2, 8192], P(None, ('col', 'mem')), may hold values from 1 to 16, as said below
- obs_value: float32 [2, 8192, 16], P(None, ('col', 'mem')), may hold values from -32 to 32
- obs_weight: float32 [2, 8192, 16], P(None, ('col', 'mem')), may hold values from 0.02 to 0.2
Outputs:
- analysis_a: bfloat16 [64, 1048576], P(None, ('col', 'mem'))
- analysis_b: bfloat16 [64, 1048576], P(None, ('col', 'mem'))
- transform: float32 [64, 64], replicated
Inputs may be any that keep to these rules, and one draw needn't show every extreme that they name: Slot s of block b of group g is an observation when s < observation_count[g, b]; for each group, every aligned run of 256 blocks holds a block with all 16 slots live.
All inputs are finite; a program needn't handle non-finite values.
Results may differ from a plain program's by a relative error of at most 0.005.
Values may be sent and summed in bfloat16 or wider, within the bound.
A program may use at most 64 MiB of HBM per device.

v0:
```python
import functools

import jax
import jax.numpy as jnp
from jax import lax
from jax.experimental import pallas as pl
from jax.experimental.pallas import tpu as pltpu
from jax.sharding import PartitionSpec as P

ITERS = 24
LANES = 128
HIGH = lax.Precision.HIGHEST
MESH = pl.DeviceIdType.MESH
ROWS = 128
CHUNK = 2048
FIRST_PART = 0.34
HX_CUTS = 4


def bits(n):
    return [1 << i for i in range(n.bit_length() - 1)]


def transform_of(gram, members):
    members = members
    g = gram[:members, :members]
    cross = gram[members : members + 1, :members]
    misfit = gram[members : members + 1, members : members + 1]
    total = gram[members + 1 : members + 2, members + 1 : members + 2]
    rows = lax.broadcasted_iota(jnp.int32, (members, members), 0)
    cols = lax.broadcasted_iota(jnp.int32, (members, members), 1)
    eye = (rows == cols).astype(jnp.float32)

    def whole(x):
        return jnp.sum(jnp.sum(x, axis=1, keepdims=True), axis=0, keepdims=True)

    def parts(x):
        hi = x.astype(jnp.bfloat16)
        rest = x - hi.astype(jnp.float32)
        mid = rest.astype(jnp.bfloat16)
        low = (rest - mid.astype(jnp.float32)).astype(jnp.bfloat16)
        return hi, mid, low

    def dot(a, b):
        total = None
        for i in range(3):
            left = jnp.concatenate(a[: 3 - i], axis=0) if i < 2 else a[0]
            out = jnp.dot(left, b[i], preferred_element_type=jnp.float32)
            for j in reversed(range(3 - i)):
                block = out[j * members : (j + 1) * members]
                total = block if total is None else total + block
        return total

    dof = members - 1.0
    scl = dof / total
    gs = scl * g
    bs = scl * cross
    rho = (1.0 + scl * misfit / dof) / (1.0 + whole(gs * eye) / dof)
    amat = dof / rho * eye + gs
    scale = jnp.sqrt(whole(amat * amat))

    def step(_, carry):
        yn, zn = carry
        yp, zp = parts(yn), parts(zn)
        tp = parts(1.5 * eye - 0.5 * dot(zp, yp))
        return dot(yp, tp), dot(tp, zp)

    _, zn = lax.fori_loop(0, ITERS, step, (amat / scale, eye))
    zp = parts(zn)
    wbar = jnp.sum(dot(zp, zp) / scale * bs, axis=1, keepdims=True)
    return jnp.sqrt(dof) * zn / jnp.sqrt(scale) + wbar


def exchange_kernel(
    nmem, ncol, sa, sb, idx, val, wgt, cnt, ra, rb, tr,
    st, idx_in, hx, cur, got, load_sem, own_sem, idx_s, idx_r, hx_s, hx_r, st_s, st_r, red_s, red_r,
):
    me = lax.axis_index("mem")
    col = lax.axis_index("col")
    mk = sa.shape[0]
    members = mk * nmem
    piece = sa.shape[1] // nmem
    width = idx.shape[1]
    half = width // 2
    states, received = (sa, sb), (ra, rb)
    chunk = min(CHUNK, piece)
    cuts = piece // chunk
    peers = [lax.rem(me + d, nmem) for d in range(1, nmem)]
    across = [{"mem": me ^ b} for b in bits(nmem)] + [{"col": col ^ b} for b in bits(ncol)]
    col_peers = [col ^ b for b in bits(ncol)]

    def cols_of(owner, start, size):
        return pl.ds(pl.multiple_of(owner * piece + start, LANES), size)

    my_rows = pl.ds(pl.multiple_of(me * mk, mk), mk)

    loads = []
    for d in range(nmem):
        owner = peers[d - 1] if d else me
        for g in range(2):
            loads.append(
                pltpu.make_async_copy(
                    states[g].at[:, cols_of(owner, 0, piece)],
                    st.at[g, :, cols_of(owner, 0, piece)],
                    load_sem.at[d, g],
                )
            )
            loads[-1].start()

    barrier = pltpu.get_barrier_semaphore()
    for p in peers:
        pl.semaphore_signal(barrier, inc=1, device_id={"mem": p}, device_id_type=MESH)
    for c in col_peers:
        pl.semaphore_signal(barrier, inc=1, device_id={"col": c}, device_id_type=MESH)
    pl.semaphore_wait(barrier, len(peers) + len(col_peers))

    index_copies = []
    for d, p in enumerate(peers):
        index_copies.append(
            pltpu.make_async_remote_copy(
                idx, idx_in.at[d], idx_s.at[d], idx_r.at[d], device_id={"mem": p}, device_id_type=MESH
            )
        )
        index_copies[-1].start()

    moves = []
    for q in range(cuts):
        for g in range(2):
            for d, p in enumerate(peers):
                n = len(moves)
                moves.append(
                    pltpu.make_async_remote_copy(
                        states[g].at[:, cols_of(p, q * chunk, chunk)],
                        received[g].at[my_rows, pl.ds(q * chunk, chunk)],
                        st_s.at[n],
                        st_r.at[n],
                        device_id={"mem": p},
                        device_id_type=MESH,
                    )
                )
    first = int(len(moves) * FIRST_PART)
    for m in moves[:first]:
        m.start()

    def gather(index, owner, start, size, put):
        lane = lax.broadcasted_iota(jnp.int32, (mk, LANES), 1) // 16

        def row(r, _):
            at = pl.multiple_of(start + r * LANES, LANES)
            g = start // half
            base = (at - g * half) * 8
            s = st[g, :, cols_of(owner, base, 8 * LANES)].astype(jnp.float32)
            ir = jnp.broadcast_to(index[:, pl.ds(at, LANES)], (mk, LANES))
            out = jnp.zeros((mk, LANES), jnp.float32)
            for j in range(8):
                picked = jnp.take_along_axis(s[:, j * LANES : (j + 1) * LANES], ir, axis=1)
                out = jnp.where(lane == j, picked, out)
            put(pl.ds(at, LANES), out.astype(jnp.bfloat16))
            return 0

        lax.fori_loop(0, size // LANES, row, 0)

    step = width // HX_CUTS
    hx_copies = []
    for d, p in enumerate(peers):
        for g in range(2):
            loads[2 * (d + 1) + g].wait()
        index_copies[nmem - 2 - d].wait()
        for h in range(HX_CUTS):

            def put(where, value):
                hx[nmem + d, :, where] = value

            gather(idx_in.at[nmem - 2 - d], p, h * step, step, put)
            hx_copies.append(
                pltpu.make_async_remote_copy(
                    hx.at[nmem + d, :, pl.ds(h * step, step)],
                    hx.at[me, :, pl.ds(h * step, step)],
                    hx_s.at[d, h],
                    hx_r.at[d, h],
                    device_id={"mem": p},
                    device_id_type=MESH,
                )
            )
            if len(hx_copies) > 1:
                hx_copies[-2].start()
    for g in range(2):
        loads[g].wait()
    keep = []
    for g in range(2):
        keep.append(
            pltpu.make_async_copy(
                st.at[g, :, cols_of(me, 0, piece)], received[g].at[my_rows, :], own_sem.at[g]
            )
        )
        keep[-1].start()

    def put_own(where, value):
        hx[me, :, where] = value

    gather(idx, me, 0, step, put_own)
    hx_copies[-1].start()
    for h in range(1, HX_CUTS):
        gather(idx, me, h * step, step, put_own)
    for c in hx_copies:
        c.wait()

    span = min(1024, half)

    def accumulate(i, acc):
        where = pl.ds(pl.multiple_of(i * span, LANES), span)
        x = jnp.concatenate([hx[m, :, where].astype(jnp.float32) for m in range(nmem)], axis=0)
        hmean = jnp.sum(x, axis=0, keepdims=True) / members
        rest = jnp.zeros((ROWS - members - 1, span), jnp.float32)
        aug = jnp.concatenate([x - hmean, val[:, where] - hmean, rest], axis=0)
        return acc + lax.dot_general(
            aug * wgt[:, where], aug, (((1,), (1,)), ((), ())), precision=HIGH,
            preferred_element_type=jnp.float32,
        )

    gram = lax.fori_loop(0, width // span, accumulate, jnp.zeros((ROWS, ROWS), jnp.float32))
    live = cnt[...].astype(jnp.float32)
    live = jnp.sum(jnp.sum(live, axis=1, keepdims=True), axis=0, keepdims=True)
    rows = lax.broadcasted_iota(jnp.int32, (ROWS, ROWS), 0)
    cols = lax.broadcasted_iota(jnp.int32, (ROWS, ROWS), 1)
    gram = jnp.where((rows == members + 1) & (cols == members + 1), live, gram)
    cur[0] = gram
    started = len(moves) if not bits(nmem) else first
    for s, peer in enumerate(across):
        copy = pltpu.make_async_remote_copy(
            cur.at[s], got.at[s], red_s.at[s], red_r.at[s], device_id=peer, device_id_type=MESH
        )
        copy.start()
        if s + 1 == len(bits(nmem)):
            for m in moves[started:]:
                m.start()
        copy.wait()
        cur[s + 1] = cur[s] + got[s]
    tr[...] = transform_of(cur[len(across)], members)
    for c in keep:
        c.wait()
    for m in moves:
        m.wait()


def exchange(state_a, state_b, idx, val, wgt, cnt):
    nmem, ncol = lax.axis_size("mem"), lax.axis_size("col")
    mk, held = state_a.shape
    piece = held // nmem
    width = idx.shape[1]
    members = mk * nmem
    steps = len(bits(nmem)) + len(bits(ncol))
    moves = 2 * (nmem - 1) * (piece // min(CHUNK, piece))
    dma = pltpu.SemaphoreType.DMA
    hbm = pl.BlockSpec(memory_space=pl.ANY)
    vmem = pl.BlockSpec(memory_space=pltpu.VMEM)
    return pl.pallas_call(
        functools.partial(exchange_kernel, nmem, ncol),
        out_shape=(
            jax.ShapeDtypeStruct((members, piece), jnp.bfloat16),
            jax.ShapeDtypeStruct((members, piece), jnp.bfloat16),
            jax.ShapeDtypeStruct((members, members), jnp.float32),
        ),
        in_specs=[hbm, hbm, vmem, vmem, vmem, vmem],
        out_specs=(hbm, hbm, vmem),
        scratch_shapes=[
            pltpu.VMEM((2, mk, held), jnp.bfloat16),
            pltpu.VMEM((nmem - 1, 1, width), jnp.int32),
            pltpu.VMEM((2 * nmem - 1, mk, width), jnp.bfloat16),
            pltpu.VMEM((steps + 1, ROWS, LANES), jnp.float32),
            pltpu.VMEM((steps, ROWS, LANES), jnp.float32),
            dma((nmem, 2)),
            dma((2,)),
            dma((nmem - 1,)),
            dma((nmem - 1,)),
            dma((nmem - 1, HX_CUTS)),
            dma((nmem - 1, HX_CUTS)),
            dma((moves,)),
            dma((moves,)),
            dma((steps,)),
            dma((steps,)),
        ],
        compiler_params=pltpu.CompilerParams(
            collective_id=0, has_side_effects=True, vmem_limit_bytes=62 * 2**20
        ),
        name="exchange",
    )(state_a, state_b, idx, val, wgt, cnt)


def apply_kernel(tr, xa, xb, oa, ob, lhs, coef):
    members = tr.shape[0]

    @pl.when(pl.program_id(0) == 0)
    def _():
        wt = tr[...].T.astype(jnp.bfloat16)
        lhs[:members, :] = wt
        lhs[members:, :] = jnp.full((16, members), 1.0 / members, jnp.bfloat16)
        coef[...] = 1.0 - jnp.sum(wt.astype(jnp.float32), axis=1, keepdims=True)

    for x, o in ((xa, oa), (xb, ob)):
        mixed = jnp.dot(lhs[...], x[...], preferred_element_type=jnp.float32)
        xmean = mixed[members : members + 1]
        o[...] = (mixed[:members] + coef[...] * xmean).astype(o.dtype)


def apply(tr, xa, xb):
    members, piece = xa.shape
    block = min(4096, piece)
    wide = pl.BlockSpec((members, block), lambda i: (0, i))
    return pl.pallas_call(
        apply_kernel,
        grid=(piece // block,),
        out_shape=(jax.ShapeDtypeStruct(xa.shape, xa.dtype),) * 2,
        in_specs=[pl.BlockSpec((members, members), lambda i: (0, 0)), wide, wide],
        out_specs=(wide, wide),
        scratch_shapes=[
            pltpu.VMEM((members + 16, members), jnp.bfloat16),
            pltpu.VMEM((members, 1), jnp.float32),
        ],
        compiler_params=pltpu.CompilerParams(dimension_semantics=("arbitrary",)),
        name="apply",
    )(tr, xa, xb)


def shards(state_a, state_b, obs_index, observation_count, obs_value, obs_weight):
    nblk, slots = obs_index.shape[1:]
    width = 2 * nblk * slots
    live = lax.broadcasted_iota(jnp.int32, obs_weight.shape, 2) < observation_count[:, :, None]
    weights = jnp.where(live, obs_weight, 0.0).reshape(1, width)
    ra, rb, transform = exchange(
        state_a, state_b, obs_index.reshape(1, width), obs_value.reshape(1, width), weights,
        observation_count,
    )
    out_a, out_b = apply(transform, ra, rb)
    return (out_a, out_b, transform)


def solution(mesh):
    return jax.shard_map(
        shards,
        mesh=mesh,
        in_specs=(
            P("mem", "col"),
            P("mem", "col"),
            P(None, ("col", "mem"), None),
            P(None, ("col", "mem")),
            P(None, ("col", "mem"), None),
            P(None, ("col", "mem"), None),
        ),
        out_specs=(P(None, ("col", "mem")), P(None, ("col", "mem")), P()),
        check_vma=False,
    )
```

profile of v0, /device:TPU:0, one launch (start us, length us, event | category | flops | bytes accessed | tf_op | source)
XLA Modules:
  0.0 133.3 jit_solution(8719758912012272181)
XLA Ops:
  0.6 0.8 fusion
  1.4 0.1 copy.14
  1.5 0.8 reshape.18.wgt
  2.3 0.9 copy.12
  3.2 0.8 reshape.16.idx
  4.0 0.9 copy.13
  4.8 0.8 reshape.17.val
  5.6 116.8 %exchange.1 = (bf16[64,32768]{1,0:T(8,128)(2,1)}, bf16[64,32768]{1,0:T(8,128)(2,1)}, f32[64,64]{1,0:T(8,128)}) custom-call(bf16[32,65536]{1,0:T(8,128)(2,1)} %sa.1, bf16[32,65536]{1,0:T(8,128)(2,1)} %sb.1, s32[1,8192]{1,0:T(1,128)} %reshape.16.idx, f32[1,8192]{1,0:T(1,128)} %reshape.17.val, f32[1,8192]{1,0:T(1,128)} %reshape.18.wgt, s32[2,256]{1,0:T(2,128)} %cnt.1), custom_call_target="tpu_custom_call" | custom-call | tf_op jit(solution)/shard_map/exchange/pallas_call | solution.py:257
  122.4 0.0 copy-start
  122.4 10.2 %apply.1 = (bf16[64,32768]{1,0:T(8,128)(2,1)}, bf16[64,32768]{1,0:T(8,128)(2,1)}) custom-call(f32[64,64]{1,0:T(8,128)} %get-tuple-element.18.tr, bf16[64,32768]{1,0:T(8,128)(2,1)} %get-tuple-element.9.xa, bf16[64,32768]{1,0:T(8,128)(2,1)} %get-tuple-element.10.xb), custom_call_target="tpu_custom_call" | custom-call | tf_op jit(solution)/shard_map/apply/pallas_call | solution.py:310
  132.7 0.0 copy-done
  132.7 0.6 copy.16
Async XLA Ops:
  122.4 10.2 %copy-start = (f32[64,64]{1,0:T(8,128)S(1)}, f32[64,64]{1,0:T(8,128)}, u32[]{:S(2)}) copy-start(f32[64,64]{1,0:T(8,128)} %get-tuple-element.18.tr) | copy-start | bytes 49156
where the time goes:
time: 134 us; the launch traced here: 133 us
  Pallas kernels  127 us (95%)
  local copies, waits for them, and re-layouts  4.81 us (4%)
    pallas_call x1, Pallas kernels, exchange(): pl.pallas_call(functools.partial(exchange_kernel, nmem, ncol), out_shape=...  117 us
    pallas_call x1, Pallas kernels, apply(): pl.pallas_call(apply_kernel, grid=(piece // block,), out_shape=(jax.Shape...  10.2 us

commit v1 on v0

v1 whole, which is shorter than its diff:
```python
import functools

import jax
import jax.numpy as jnp
from jax import lax
from jax.experimental import pallas as pl
from jax.experimental.pallas import tpu as pltpu
from jax.sharding import PartitionSpec as P

ITERS = 24
LANES = 128
HIGH = lax.Precision.HIGHEST
MESH = pl.DeviceIdType.MESH
ROWS = 128
UNIT = 1024
LATE = 0.25
AHEAD = 0.0625
EARLY_UNITS = 2
LATE_UNITS = 2
FIRST = 3
TILE = 2048


def bits(n):
    return [1 << i for i in range(n.bit_length() - 1)]


def transform_of(gram, members):
    g = gram[:members, :members]
    cross = gram[members : members + 1, :members]
    misfit = gram[members : members + 1, members : members + 1]
    total = gram[members + 1 : members + 2, members + 1 : members + 2]
    rows = lax.broadcasted_iota(jnp.int32, (members, members), 0)
    cols = lax.broadcasted_iota(jnp.int32, (members, members), 1)
    eye = (rows == cols).astype(jnp.float32)

    def whole(x):
        return jnp.sum(jnp.sum(x, axis=1, keepdims=True), axis=0, keepdims=True)

    def parts(x):
        hi = x.astype(jnp.bfloat16)
        rest = x - hi.astype(jnp.float32)
        mid = rest.astype(jnp.bfloat16)
        low = (rest - mid.astype(jnp.float32)).astype(jnp.bfloat16)
        return hi, mid, low

    def dot(a, b):
        total = None
        for i in range(3):
            left = jnp.concatenate(a[: 3 - i], axis=0) if i < 2 else a[0]
            out = jnp.dot(left, b[i], preferred_element_type=jnp.float32)
            for j in reversed(range(3 - i)):
                block = out[j * members : (j + 1) * members]
                total = block if total is None else total + block
        return total

    dof = members - 1.0
    scl = dof / total
    gs = scl * g
    bs = scl * cross
    rho = (1.0 + scl * misfit / dof) / (1.0 + whole(gs * eye) / dof)
    amat = dof / rho * eye + gs
    scale = jnp.sqrt(whole(amat * amat))

    def step(_, carry):
        yn, zn = carry
        yp, zp = parts(yn), parts(zn)
        tp = parts(1.5 * eye - 0.5 * dot(zp, yp))
        return dot(yp, tp), dot(tp, zp)

    _, zn = lax.fori_loop(0, ITERS, step, (amat / scale, eye))
    zp = parts(zn)
    wbar = jnp.sum(dot(zp, zp) / scale * bs, axis=1, keepdims=True)
    return jnp.sqrt(dof) * zn / jnp.sqrt(scale) + wbar


def plan(piece):
    units = piece // UNIT
    late = max(1, round(units * LATE))
    step = EARLY_UNITS if (units - late) % EARLY_UNITS == 0 else 1
    early = units - late
    sizes = []
    while sum(sizes) < late:
        sizes.append(min(LATE_UNITS, late - sum(sizes)))
    ahead, count = 0, 0
    while count < len(sizes) and ahead + sizes[count] <= max(1, round(units * AHEAD)):
        ahead += sizes[count]
        count += 1
    return units, early, step, sizes, count


def exchange_kernel(
    nmem, ncol, sa, sb, idx_hbm, val_hbm, wgt_hbm, cnt_hbm, oa, ob, tr,
    idx, val, wgt, cnt, table_sem, stage, idx_f, val_f, wgt_f, idx_tx, idx_in, tx, hx, cur, got, lhs,
    own_sem, stage_sem, idx_s, idx_r, hx_s, hx_r, st_s, st_r, red_s, red_r,
):
    me = lax.axis_index("mem")
    col = lax.axis_index("col")
    mk = sa.shape[0]
    members = mk * nmem
    piece = sa.shape[1] // nmem
    nblk = idx.shape[2]
    units, early, step, late_sizes, ahead = plan(piece)
    late = units - early
    state, out = (sa, sb), (oa, ob)
    peers = [lax.rem(me + d, nmem) for d in range(1, nmem)]
    across = [{"mem": me ^ b} for b in bits(nmem)] + [{"col": col ^ b} for b in bits(ncol)]

    def cols_of(owner, unit, size):
        return pl.ds(pl.multiple_of(owner * piece + unit * UNIT, LANES), size * UNIT)

    my_rows = pl.ds(pl.multiple_of(me * mk, mk), mk)

    loads = []
    for d, p in enumerate(peers):
        for g in range(2):
            loads.append(
                pltpu.make_async_copy(
                    state[g].at[:, cols_of(p, early, late)], stage.at[d, g], stage_sem.at[d, g]
                )
            )
    own = []
    for g in range(2):
        own.append(
            pltpu.make_async_copy(
                state[g].at[:, cols_of(me, 0, units)], out[g].at[my_rows, :], own_sem.at[g]
            )
        )
    tables = []
    for n, (a, b) in enumerate(((idx_hbm, idx), (val_hbm, val), (wgt_hbm, wgt), (cnt_hbm, cnt))):
        tables.append(pltpu.make_async_copy(a, b, table_sem.at[n]))
    for c in tables + loads + own:
        c.start()

    barrier = pltpu.get_barrier_semaphore()
    for p in peers:
        pl.semaphore_signal(barrier, inc=1, device_id={"mem": p}, device_id_type=MESH)
    for b in bits(ncol):
        pl.semaphore_signal(barrier, inc=1, device_id={"col": col ^ b}, device_id_type=MESH)
    pl.semaphore_wait(barrier, len(peers) + len(bits(ncol)))

    def move(slot, unit, size, g, d):
        return pltpu.make_async_remote_copy(
            state[g].at[:, cols_of(peers[d], unit, size)],
            out[g].at[my_rows, pl.ds(pl.multiple_of(unit * UNIT, LANES), size * UNIT)],
            st_s.at[slot],
            st_r.at[slot],
            device_id={"mem": peers[d]},
            device_id_type=MESH,
        )

    each = [(g, d) for g in range(2) for d in range(nmem - 1)]
    chunks = early // step

    def early_moves(q):
        return [move(q * len(each) + n, q * step, step, g, d) for n, (g, d) in enumerate(each)]

    late_moves = []
    at = early
    for n, size in enumerate(late_sizes):
        slot = (chunks + n) * len(each)
        late_moves.append((at, size, [move(slot + k, at, size, g, d) for k, (g, d) in enumerate(each)]))
        at += size

    def start_early(q, _):
        for m in early_moves(q):
            m.start()
        return 0

    first = min(FIRST, chunks)
    start_early(0, 0)

    for c in tables:
        c.wait()
    slot_of = lax.broadcasted_iota(jnp.int32, (16, nblk), 0)
    diag = (
        lax.broadcasted_iota(jnp.int32, (8, LANES), 0)
        == lax.broadcasted_iota(jnp.int32, (8, LANES), 1) // 16
    )

    def flat(x):
        x = jnp.concatenate([x] * 8, axis=0).T.reshape(units, 8, LANES)
        return jnp.sum(jnp.where(diag[None], x, 0.0), axis=1)

    for g in range(2):
        rows = flat(idx[g].astype(jnp.float32)).astype(jnp.int32)
        idx_f[g] = rows
        idx_tx[g] = rows[early:]
    for g in range(2):
        live = slot_of < cnt[g : g + 1, :]
        wgt_f[g] = flat(jnp.where(live, wgt[g], 0.0))
        val_f[g] = flat(val[g])

    idx_copies = []
    for d, p in enumerate(peers):
        idx_copies.append(
            pltpu.make_async_remote_copy(
                idx_tx, idx_in.at[d], idx_s.at[d], idx_r.at[d], device_id={"mem": p}, device_id_type=MESH
            )
        )
        idx_copies[-1].start()
    lax.fori_loop(1, first, start_early, 0)

    def gather(s, index):
        rows = s.shape[0]
        lane = lax.broadcasted_iota(jnp.int32, (rows, LANES), 1) // 16
        s = s.astype(jnp.float32)
        index = jnp.broadcast_to(index, (rows, LANES))
        picked = None
        for j in range(8):
            here = jnp.take_along_axis(s[:, j * LANES : (j + 1) * LANES], index, axis=1)
            picked = here if picked is None else jnp.where(lane == j, here, picked)
        return picked

    def lanes_of(unit):
        return pl.ds(pl.multiple_of(unit * LANES, LANES), LANES)

    def unit_cols(unit):
        return pl.ds(pl.multiple_of(unit * UNIT, LANES), UNIT)

    for c in loads:
        c.wait()
    hx_copies = []
    for d, p in enumerate(peers):
        src = nmem - 2 - d
        idx_copies[src].wait()
        for g in range(2):

            def send_row(u, _):
                picked = gather(stage[d, g, :, unit_cols(u)], idx_in[src, g, pl.ds(u, 1), :])
                tx[d, g, :, lanes_of(u)] = picked.astype(jnp.bfloat16)
                return 0

            lax.fori_loop(0, late, send_row, 0)
        hx_copies.append(
            pltpu.make_async_remote_copy(
                tx.at[d], hx.at[me], hx_s.at[d], hx_r.at[d], device_id={"mem": p}, device_id_type=MESH
            )
        )
    for c in own:
        c.wait()
    for g in range(2):

        def own_row(u, _):
            picked = gather(out[g][my_rows, unit_cols(early + u)], idx_f[g, pl.ds(early + u, 1), :])
            hx[me, g, :, lanes_of(u)] = picked.astype(jnp.bfloat16)
            return 0

        lax.fori_loop(0, late, own_row, 0)
    for c in hx_copies:
        c.start()
    lax.fori_loop(first, chunks, start_early, 0)
    for _, _, ms in late_moves[:ahead]:
        for m in ms:
            m.start()

    def product(acc, x, value, weight):
        hmean = jnp.sum(x, axis=0, keepdims=True) / members
        rest = jnp.zeros((ROWS - members - 1, x.shape[1]), jnp.float32)
        aug = jnp.concatenate([x - hmean, value - hmean, rest], axis=0)
        return acc + lax.dot_general(
            aug * weight, aug, (((1,), (1,)), ((), ())), precision=HIGH,
            preferred_element_type=jnp.float32,
        )

    def early_sum(q, acc):
        for m in early_moves(q):
            m.wait_recv()
        xs, vs, ws = [], [], []
        for g in range(2):
            for k in range(step):
                u = q * step + k
                xs.append(gather(out[g][:, unit_cols(u)], idx_f[g, pl.ds(u, 1), :]))
                vs.append(val_f[g, pl.ds(u, 1), :])
                ws.append(wgt_f[g, pl.ds(u, 1), :])
        return product(acc, *(jnp.concatenate(t, axis=1) for t in (xs, vs, ws)))

    acc = lax.fori_loop(0, chunks - 1, early_sum, jnp.zeros((ROWS, ROWS), jnp.float32))
    for c in hx_copies:
        c.wait()

    def late_sum(u, acc):
        x, value, weight = [], [], []
        for g in range(2):
            x.append(
                jnp.concatenate([hx[m, g, :, lanes_of(u)].astype(jnp.float32) for m in range(nmem)], axis=0)
            )
            value.append(val_f[g, pl.ds(early + u, 1), :])
            weight.append(wgt_f[g, pl.ds(early + u, 1), :])
        return product(acc, *(jnp.concatenate(t, axis=1) for t in (x, value, weight)))

    acc = lax.fori_loop(0, late, late_sum, acc)
    acc = early_sum(chunks - 1, acc)

    live = cnt[...].astype(jnp.float32)
    live = jnp.sum(jnp.sum(live, axis=1, keepdims=True), axis=0, keepdims=True)
    used = cur.shape[1]
    rows = lax.broadcasted_iota(jnp.int32, (used, LANES), 0)
    cols = lax.broadcasted_iota(jnp.int32, (used, LANES), 1)
    cur[0] = jnp.where((rows == members + 1) & (cols == members + 1), live, acc[:used])
    started = ahead
    for s, peer in enumerate(across):
        copy = pltpu.make_async_remote_copy(
            cur.at[s], got.at[s], red_s.at[s], red_r.at[s], device_id=peer, device_id_type=MESH
        )
        copy.start()
        if s + 1 == len(bits(nmem)):
            for _, _, ms in late_moves[started:]:
                for m in ms:
                    m.start()
        copy.wait()
        cur[s + 1] = cur[s] + got[s]
    if not bits(nmem):
        for _, _, ms in late_moves[started:]:
            for m in ms:
                m.start()
    weights = transform_of(cur[len(across)], members)
    tr[...] = weights
    wt = weights.T.astype(jnp.bfloat16)
    lhs[:members, :] = wt
    lhs[members:, :] = jnp.full((16, members), 1.0 / members, jnp.bfloat16)
    coef = 1.0 - jnp.sum(wt.astype(jnp.float32), axis=1, keepdims=True)

    def mix(at, size):
        where = pl.ds(pl.multiple_of(at, LANES), size)
        for g in range(2):
            mixed = jnp.dot(lhs[...], out[g][:, where], preferred_element_type=jnp.float32)
            xmean = mixed[members : members + 1]
            out[g][:, where] = (mixed[:members] + coef * xmean).astype(jnp.bfloat16)

    tile = TILE if (early * UNIT) % TILE == 0 else UNIT

    def mix_early(i, _):
        mix(i * tile, tile)
        return 0

    lax.fori_loop(0, early * UNIT // tile, mix_early, 0)
    for at, size, ms in late_moves:
        for m in ms:
            m.wait_recv()
        mix(at * UNIT, size * UNIT)

    def end_early(q, _):
        for m in early_moves(q):
            m.wait_send()
        return 0

    lax.fori_loop(0, chunks, end_early, 0)
    for _, _, ms in late_moves:
        for m in ms:
            m.wait_send()


def exchange(state_a, state_b, idx, val, wgt, cnt):
    nmem, ncol = lax.axis_size("mem"), lax.axis_size("col")
    mk, held = state_a.shape
    piece = held // nmem
    members = mk * nmem
    units, early, step, late_sizes, ahead = plan(piece)
    late = units - early
    steps = len(bits(nmem)) + len(bits(ncol))
    moves = 2 * (nmem - 1) * (early // step + len(late_sizes))
    used = (members + 2 + 7) // 8 * 8
    dma = pltpu.SemaphoreType.DMA
    hbm = pl.BlockSpec(memory_space=pltpu.HBM)
    vmem = pl.BlockSpec(memory_space=pltpu.VMEM)
    return pl.pallas_call(
        functools.partial(exchange_kernel, nmem, ncol),
        out_shape=(
            pltpu.VMEM((members, piece), jnp.bfloat16),
            pltpu.VMEM((members, piece), jnp.bfloat16),
            pltpu.VMEM((members, members), jnp.float32),
        ),
        in_specs=[hbm] * 6,
        out_specs=(vmem, vmem, vmem),
        scratch_shapes=[
            *(pltpu.VMEM(x.shape, x.dtype) for x in (idx, val, wgt, cnt)),
            dma((4,)),
            pltpu.VMEM((nmem - 1, 2, mk, late * UNIT), jnp.bfloat16),
            pltpu.VMEM((2, units, LANES), jnp.int32),
            pltpu.VMEM((2, units, LANES), jnp.float32),
            pltpu.VMEM((2, units, LANES), jnp.float32),
            pltpu.VMEM((2, late, LANES), jnp.int32),
            pltpu.VMEM((nmem - 1, 2, late, LANES), jnp.int32),
            pltpu.VMEM((nmem - 1, 2, mk, late * LANES), jnp.bfloat16),
            pltpu.VMEM((nmem, 2, mk, late * LANES), jnp.bfloat16),
            pltpu.VMEM((steps + 1, used, LANES), jnp.float32),
            pltpu.VMEM((steps, used, LANES), jnp.float32),
            pltpu.VMEM((members + 16, members), jnp.bfloat16),
            dma((2,)),
            dma((nmem - 1, 2)),
            dma((nmem - 1,)),
            dma((nmem - 1,)),
            dma((nmem - 1,)),
            dma((nmem - 1,)),
            dma((moves,)),
            dma((moves,)),
            dma((steps,)),
            dma((steps,)),
        ],
        compiler_params=pltpu.CompilerParams(
            collective_id=0, has_side_effects=True, vmem_limit_bytes=40 * 2**20
        ),
        name="exchange",
    )(*(pltpu.with_memory_space_constraint(x, pltpu.HBM) for x in (state_a, state_b, idx, val, wgt, cnt)))


def write_kernel(parts, xa, xb, tr, oa, ob, ot, sems, tr_sem):
    width = xa.shape[1] // parts
    copies = [pltpu.make_async_copy(tr, ot, tr_sem)]
    for i in range(parts):
        for g, (x, o) in enumerate(((xa, oa), (xb, ob))):
            where = pl.ds(i * width, width)
            copies.append(pltpu.make_async_copy(x.at[:, where], o.at[:, where], sems.at[g, i]))
    for c in copies:
        c.start()
    for c in copies:
        c.wait()


def write(xa, xb, tr):
    parts = 4
    vmem = pl.BlockSpec(memory_space=pltpu.VMEM)
    hbm = pl.BlockSpec(memory_space=pltpu.HBM)
    return pl.pallas_call(
        functools.partial(write_kernel, parts),
        out_shape=tuple(jax.ShapeDtypeStruct(x.shape, x.dtype) for x in (xa, xb, tr)),
        in_specs=[vmem, vmem, vmem],
        out_specs=(hbm, hbm, hbm),
        scratch_shapes=[pltpu.SemaphoreType.DMA((2, parts)), pltpu.SemaphoreType.DMA],
        compiler_params=pltpu.CompilerParams(vmem_limit_bytes=40 * 2**20),
        name="write",
    )(xa, xb, tr)


def shards(state_a, state_b, obs_index, observation_count, obs_value, obs_weight):
    tables = [jnp.transpose(x, (0, 2, 1)) for x in (obs_index, obs_value, obs_weight)]
    return write(*exchange(state_a, state_b, *tables, observation_count))


def solution(mesh):
    return jax.shard_map(
        shards,
        mesh=mesh,
        in_specs=(
            P("mem", "col"),
            P("mem", "col"),
            P(None, ("col", "mem"), None),
            P(None, ("col", "mem")),
            P(None, ("col", "mem"), None),
            P(None, ("col", "mem"), None),
        ),
        out_specs=(P(None, ("col", "mem")), P(None, ("col", "mem")), P()),
        check_vma=False,
    )
```

time: 134 us -> 114 us (0.85)
  Pallas kernels: 127 us -> 113 us
  local copies, waits for them, and re-layouts: 4.81 us -> 0 us
    pallas_call x1, Pallas kernels: 117 us -> 110 us  [exchange(): pl.pallas_call(functools.partial(exchange_kernel, nmem, ncol), out_shape=...]
    pallas_call x1, Pallas kernels: 10.2 us -> 3.39 us  [write(): pl.pallas_call(functools.partial(write_kernel, parts), out_shape=tuple((j...]
    unnamed x5 -> x0, local copies, waits for them, and re-layouts: 2.37 us -> none
    reshape x3 -> x0, local copies, waits for them, and re-layouts: 2.31 us -> none  [the longest x1 0.77 us: shards(): weights = jnp.where(live, obs_weight, 0.0).reshape(1, width)]
where the time goes in v1:
time: 114 us
  Pallas kernels  113 us (99%)
    pallas_call x1, Pallas kernels, exchange(): pl.pallas_call(functools.partial(exchange_kernel, nmem, ncol), out_shape=...  110 us
    pallas_call x1, Pallas kernels, write(): pl.pallas_call(functools.partial(write_kernel, parts), out_shape=tuple((j...  3.39 us

profile of v1, /device:TPU:0, one launch (start us, length us, event | category | flops | bytes accessed | tf_op | source)
XLA Modules:
  0.0 113.8 jit_solution(16378255840343344170)
XLA Ops:
  0.6 109.8 %exchange.1 = (bf16[64,32768]{1,0:T(8,128)(2,1)S(1)}, bf16[64,32768]{1,0:T(8,128)(2,1)S(1)}, f32[64,64]{1,0:T(8,128)S(1)}) custom-call(bf16[32,65536]{1,0:T(8,128)(2,1)} %sa.1, bf16[32,65536]{1,0:T(8,128)(2,1)} %sb.1, s32[2,16,256]{2,1,0:T(8,128)} %bitcast.3, f32[2,16,256]{2,1,0:T(8,128)} %bitcast.4, f32[2,16,256]{2,1,0:T(8,128)} %bitcast.5, s32[2,256]{1,0:T(2,128)} %cnt_hbm.1), custom_call_target="tpu_custom_call" | custom-call | tf_op jit(solution)/shard_map/exchange/pallas_call | solution.py:367
  110.4 3.4 %write.1 = (bf16[64,32768]{1,0:T(8,128)(2,1)}, bf16[64,32768]{1,0:T(8,128)(2,1)}, f32[64,64]{1,0:T(8,128)}) custom-call(bf16[64,32768]{1,0:T(8,128)(2,1)S(1)} %get-tuple-element.6.xa, bf16[64,32768]{1,0:T(8,128)(2,1)S(1)} %get-tuple-element.7.xb, f32[64,64]{1,0:T(8,128)S(1)} %get-tuple-element.8.tr), custom_call_target="tpu_custom_call" | custom-call | tf_op jit(solution)/shard_map/write/pallas_call | solution.py:425

commit v2 on v1

--- a/solution.py
+++ b/solution.py
@@ -13,10 +13,8 @@
 MESH = pl.DeviceIdType.MESH
 ROWS = 128
 UNIT = 1024
-LATE = 0.25
-AHEAD = 0.0625
-EARLY_UNITS = 2
-LATE_UNITS = 2
+LATE = 0.3125
+STEP = 2
 FIRST = 3
 TILE = 2048
 
@@ -76,23 +74,27 @@
 
 def plan(piece):
     units = piece // UNIT
-    late = max(1, round(units * LATE))
-    step = EARLY_UNITS if (units - late) % EARLY_UNITS == 0 else 1
-    early = units - late
-    sizes = []
-    while sum(sizes) < late:
-        sizes.append(min(LATE_UNITS, late - sum(sizes)))
-    ahead, count = 0, 0
-    while count < len(sizes) and ahead + sizes[count] <= max(1, round(units * AHEAD)):
-        ahead += sizes[count]
-        count += 1
-    return units, early, step, sizes, count
+    step = STEP if units % STEP == 0 else 1
+    late = max(1, round(units // step * LATE))
+    return units, step, units // step - late, late
+
+
+def sum_rounds(nmem, ncol):
+    aside = 4 if ncol > 4 else 0
+    gens = [(b, aside) for b in bits(nmem)] + [(0, b) for b in bits(ncol) if b > 1]
+    rounds = []
+    for i in range(0, len(gens), 2):
+        pair = gens[i : i + 2]
+        if len(pair) == 2:
+            pair.append((pair[0][0] ^ pair[1][0], pair[0][1] ^ pair[1][1]))
+        rounds.append(pair)
+    return rounds
 
 
 def exchange_kernel(
     nmem, ncol, sa, sb, idx_hbm, val_hbm, wgt_hbm, cnt_hbm, oa, ob, tr,
-    idx, val, wgt, cnt, table_sem, stage, idx_f, val_f, wgt_f, idx_tx, idx_in, tx, hx, cur, got, lhs,
-    own_sem, stage_sem, idx_s, idx_r, hx_s, hx_r, st_s, st_r, red_s, red_r,
+    idx, val, wgt, cnt, table_sem, stage, idx_f, val_f, wgt_f, idx_tx, idx_in, tx, hx, cur, got, res, lhs,
+    own_sem, stage_sem, idx_s, idx_r, hx_s, hx_r, st_s, st_r, red_s, red_r, pair_s, pair_r, known,
 ):
     me = lax.axis_index("mem")
     col = lax.axis_index("col")
@@ -100,11 +102,19 @@
     members = mk * nmem
     piece = sa.shape[1] // nmem
     nblk = idx.shape[2]
-    units, early, step, late_sizes, ahead = plan(piece)
+    units, step, chunks, late_chunks = plan(piece)
+    early = chunks * step
     late = units - early
     state, out = (sa, sb), (oa, ob)
     peers = [lax.rem(me + d, nmem) for d in range(1, nmem)]
-    across = [{"mem": me ^ b} for b in bits(nmem)] + [{"col": col ^ b} for b in bits(ncol)]
+    rounds = sum_rounds(nmem, ncol)
+    greeted = sorted({p for r in rounds for p in r if p[1]})
+    paired = ncol > 1
+    mate = {"col": col ^ 1}
+    hub = lax.rem(col, 2) == 0
+
+    def partner(p):
+        return {"mem": me ^ p[0], "col": col ^ p[1]}
 
     def cols_of(owner, unit, size):
         return pl.ds(pl.multiple_of(owner * piece + unit * UNIT, LANES), size * UNIT)
@@ -129,15 +139,24 @@
     tables = []
     for n, (a, b) in enumerate(((idx_hbm, idx), (val_hbm, val), (wgt_hbm, wgt), (cnt_hbm, cnt))):
         tables.append(pltpu.make_async_copy(a, b, table_sem.at[n]))
-    for c in tables + loads + own:
+    for c in tables:
         c.start()
 
     barrier = pltpu.get_barrier_semaphore()
     for p in peers:
         pl.semaphore_signal(barrier, inc=1, device_id={"mem": p}, device_id_type=MESH)
-    for b in bits(ncol):
-        pl.semaphore_signal(barrier, inc=1, device_id={"col": col ^ b}, device_id_type=MESH)
-    pl.semaphore_wait(barrier, len(peers) + len(bits(ncol)))
+    @pl.when(hub)
+    def _():
+        for p in greeted:
+            pl.semaphore_signal(barrier, inc=1, device_id=partner(p), device_id_type=MESH)
+        pl.semaphore_wait(barrier, len(peers) + len(greeted) + paired)
+        if paired:
+            pl.semaphore_signal(known, inc=1, device_id=mate, device_id_type=MESH)
+
+    @pl.when(jnp.logical_not(hub))
+    def _():
+        pl.semaphore_signal(barrier, inc=1, device_id=mate, device_id_type=MESH)
+        pl.semaphore_wait(barrier, len(peers))
 
     def move(slot, unit, size, g, d):
         return pltpu.make_async_remote_copy(
@@ -150,25 +169,19 @@
         )
 
     each = [(g, d) for g in range(2) for d in range(nmem - 1)]
-    chunks = early // step
-
-    def early_moves(q):
+
+    def moves(q):
         return [move(q * len(each) + n, q * step, step, g, d) for n, (g, d) in enumerate(each)]
 
-    late_moves = []
-    at = early
-    for n, size in enumerate(late_sizes):
-        slot = (chunks + n) * len(each)
-        late_moves.append((at, size, [move(slot + k, at, size, g, d) for k, (g, d) in enumerate(each)]))
-        at += size
-
-    def start_early(q, _):
-        for m in early_moves(q):
+    def start(q, _):
+        for m in moves(q):
             m.start()
         return 0
 
     first = min(FIRST, chunks)
-    start_early(0, 0)
+    start(0, 0)
+    for c in loads + own:
+        c.start()
 
     for c in tables:
         c.wait()
@@ -199,7 +212,7 @@
             )
         )
         idx_copies[-1].start()
-    lax.fori_loop(1, first, start_early, 0)
+    lax.fori_loop(1, first, start, 0)
 
     def gather(s, index):
         rows = s.shape[0]
@@ -249,10 +262,7 @@
         lax.fori_loop(0, late, own_row, 0)
     for c in hx_copies:
         c.start()
-    lax.fori_loop(first, chunks, start_early, 0)
-    for _, _, ms in late_moves[:ahead]:
-        for m in ms:
-            m.start()
+    lax.fori_loop(first, chunks + late_chunks, start, 0)
 
     def product(acc, x, value, weight):
         hmean = jnp.sum(x, axis=0, keepdims=True) / members
@@ -264,7 +274,7 @@
         )
 
     def early_sum(q, acc):
-        for m in early_moves(q):
+        for m in moves(q):
             m.wait_recv()
         xs, vs, ws = [], [], []
         for g in range(2):
@@ -294,27 +304,56 @@
 
     live = cnt[...].astype(jnp.float32)
     live = jnp.sum(jnp.sum(live, axis=1, keepdims=True), axis=0, keepdims=True)
-    used = cur.shape[1]
+    used = res.shape[0]
     rows = lax.broadcasted_iota(jnp.int32, (used, LANES), 0)
     cols = lax.broadcasted_iota(jnp.int32, (used, LANES), 1)
-    cur[0] = jnp.where((rows == members + 1) & (cols == members + 1), live, acc[:used])
-    started = ahead
-    for s, peer in enumerate(across):
-        copy = pltpu.make_async_remote_copy(
-            cur.at[s], got.at[s], red_s.at[s], red_r.at[s], device_id=peer, device_id_type=MESH
+    acc = jnp.where((rows == members + 1) & (cols == members + 1), live, acc[:used])
+
+    def to_mate(n, src, dst):
+        return pltpu.make_async_remote_copy(
+            src, dst, pair_s.at[n], pair_r.at[n], device_id=mate, device_id_type=MESH
         )
-        copy.start()
-        if s + 1 == len(bits(nmem)):
-            for _, _, ms in late_moves[started:]:
-                for m in ms:
-                    m.start()
-        copy.wait()
-        cur[s + 1] = cur[s] + got[s]
-    if not bits(nmem):
-        for _, _, ms in late_moves[started:]:
-            for m in ms:
-                m.start()
-    weights = transform_of(cur[len(across)], members)
+
+    @pl.when(hub)
+    def _():
+        total = acc
+        if paired:
+            to_mate(0, res, got.at[0]).wait_recv()
+            total = total + got[0]
+        slot = 1
+        for n, r in enumerate(rounds):
+            cur[n] = total
+            copies = []
+            for p in r:
+                copies.append(
+                    pltpu.make_async_remote_copy(
+                        cur.at[n], got.at[slot + len(copies)],
+                        red_s.at[slot + len(copies)], red_r.at[slot + len(copies)],
+                        device_id=partner(p), device_id_type=MESH,
+                    )
+                )
+            for c in copies:
+                c.start()
+            for c in copies:
+                c.wait()
+            total = total + got[slot]
+            if len(r) == 3:
+                total = total + (got[slot + 1] + got[slot + 2])
+            slot += len(r)
+        res[...] = total
+        if paired:
+            to_mate(1, res, res).start()
+
+    @pl.when(jnp.logical_not(hub))
+    def _():
+        cur[0] = acc
+        pl.semaphore_wait(known, 1)
+        send = to_mate(0, cur.at[0], got.at[0])
+        send.start()
+        send.wait_send()
+        to_mate(1, res, res).wait_recv()
+
+    weights = transform_of(res[...], members)
     tr[...] = weights
     wt = weights.T.astype(jnp.bfloat16)
     lhs[:members, :] = wt
@@ -335,20 +374,26 @@
         return 0
 
     lax.fori_loop(0, early * UNIT // tile, mix_early, 0)
-    for at, size, ms in late_moves:
-        for m in ms:
+
+    def mix_late(q, _):
+        for m in moves(q):
             m.wait_recv()
-        mix(at * UNIT, size * UNIT)
-
-    def end_early(q, _):
-        for m in early_moves(q):
+        mix(q * step * UNIT, step * UNIT)
+        return 0
+
+    lax.fori_loop(chunks, chunks + late_chunks, mix_late, 0)
+
+    def end(q, _):
+        for m in moves(q):
             m.wait_send()
         return 0
 
-    lax.fori_loop(0, chunks, end_early, 0)
-    for _, _, ms in late_moves:
-        for m in ms:
-            m.wait_send()
+    lax.fori_loop(0, chunks + late_chunks, end, 0)
+
+    @pl.when(hub)
+    def _():
+        if paired:
+            to_mate(1, res, res).wait_send()
 
 
 def exchange(state_a, state_b, idx, val, wgt, cnt):
@@ -356,10 +401,11 @@
     mk, held = state_a.shape
     piece = held // nmem
     members = mk * nmem
-    units, early, step, late_sizes, ahead = plan(piece)
-    late = units - early
-    steps = len(bits(nmem)) + len(bits(ncol))
-    moves = 2 * (nmem - 1) * (early // step + len(late_sizes))
+    units, step, chunks, late_chunks = plan(piece)
+    late = late_chunks * step
+    rounds = sum_rounds(nmem, ncol)
+    slots = 1 + sum(len(r) for r in rounds)
+    moves = 2 * (nmem - 1) * (chunks + late_chunks)
     used = (members + 2 + 7) // 8 * 8
     dma = pltpu.SemaphoreType.DMA
     hbm = pl.BlockSpec(memory_space=pltpu.HBM)
@@ -384,8 +430,9 @@
             pltpu.VMEM((nmem - 1, 2, late, LANES), jnp.int32),
             pltpu.VMEM((nmem - 1, 2, mk, late * LANES), jnp.bfloat16),
             pltpu.VMEM((nmem, 2, mk, late * LANES), jnp.bfloat16),
-            pltpu.VMEM((steps + 1, used, LANES), jnp.float32),
-            pltpu.VMEM((steps, used, LANES), jnp.float32),
+            pltpu.VMEM((max(1, len(rounds)), used, LANES), jnp.float32),
+            pltpu.VMEM((slots, used, LANES), jnp.float32),
+            pltpu.VMEM((used, LANES), jnp.float32),
             pltpu.VMEM((members + 16, members), jnp.bfloat16),
             dma((2,)),
             dma((nmem - 1, 2)),
@@ -395,8 +442,11 @@
             dma((nmem - 1,)),
             dma((moves,)),
             dma((moves,)),
-            dma((steps,)),
-            dma((steps,)),
+            dma((slots,)),
+            dma((slots,)),
+            dma((2,)),
+            dma((2,)),
+            pltpu.SemaphoreType.REGULAR,
         ],
         compiler_params=pltpu.CompilerParams(
             collective_id=0, has_side_effects=True, vmem_limit_bytes=40 * 2**20

time: 114 us -> 104 us (0.912)
  Pallas kernels: 113 us -> 103 us
    pallas_call x1, Pallas kernels: 110 us -> 99.6 us  [exchange(): pl.pallas_call(functools.partial(exchange_kernel, nmem, ncol), out_shape=...]
where the time goes in v2:
time: 104 us
  Pallas kernels  103 us (99%)
    pallas_call x1, Pallas kernels, exchange(): pl.pallas_call(functools.partial(exchange_kernel, nmem, ncol), out_shape=...  99.6 us
    pallas_call x1, Pallas kernels, write(): pl.pallas_call(functools.partial(write_kernel, parts), out_shape=tuple((j...  3.39 us

profile of v2, /device:TPU:0, one launch (start us, length us, event | category | flops | bytes accessed | tf_op | source)
XLA Modules:
  0.0 103.6 jit_solution(8875391375198126253)
XLA Ops:
  0.6 99.6 %exchange.1 = (bf16[64,32768]{1,0:T(8,128)(2,1)S(1)}, bf16[64,32768]{1,0:T(8,128)(2,1)S(1)}, f32[64,64]{1,0:T(8,128)S(1)}) custom-call(bf16[32,65536]{1,0:T(8,128)(2,1)} %sa.1, bf16[32,65536]{1,0:T(8,128)(2,1)} %sb.1, s32[2,16,256]{2,1,0:T(8,128)} %bitcast.3, f32[2,16,256]{2,1,0:T(8,128)} %bitcast.4, f32[2,16,256]{2,1,0:T(8,128)} %bitcast.5, s32[2,256]{1,0:T(2,128)} %cnt_hbm.1), custom_call_target="tpu_custom_call" | custom-call | tf_op jit(solution)/shard_map/exchange/pallas_call | solution.py:413
  100.3 3.4 %write.1 = (bf16[64,32768]{1,0:T(8,128)(2,1)}, bf16[64,32768]{1,0:T(8,128)(2,1)}, f32[64,64]{1,0:T(8,128)}) custom-call(bf16[64,32768]{1,0:T(8,128)(2,1)S(1)} %get-tuple-element.6.xa, bf16[64,32768]{1,0:T(8,128)(2,1)S(1)} %get-tuple-element.7.xb, f32[64,64]{1,0:T(8,128)S(1)} %get-tuple-element.8.tr), custom_call_target="tpu_custom_call" | custom-call | tf_op jit(solution)/shard_map/write/pallas_call | solution.py:475

commit v3 on v2

--- a/solution.py
+++ b/solution.py
@@ -14,20 +14,29 @@
 ROWS = 128
 UNIT = 1024
 LATE = 0.3125
-STEP = 2
-FIRST = 3
-TILE = 2048
+FIRST = 12
+EARLY_SIZES = (1, 2, 4)
+LATE_SIZES = (2, 4)
+WIDE = 6144
 
 
 def bits(n):
     return [1 << i for i in range(n.bit_length() - 1)]
 
 
-def transform_of(gram, members):
-    g = gram[:members, :members]
-    cross = gram[members : members + 1, :members]
-    misfit = gram[members : members + 1, members : members + 1]
-    total = gram[members + 1 : members + 2, members + 1 : members + 2]
+def pack(sums, live, members):
+    height = members * members // LANES
+    rows = [sums[i : i + height, :members] for i in range(0, members, height)]
+    lane = lax.broadcasted_iota(jnp.int32, (1, LANES), 1)
+    last = jnp.where(lane == members + 1, live, sums[members : members + 1])
+    return jnp.concatenate([jnp.concatenate(rows, axis=1), last, jnp.zeros((7, LANES), jnp.float32)], axis=0)
+
+
+def transform_of(packed, members):
+    height = members * members // LANES
+    g = jnp.concatenate([packed[:height, i : i + members] for i in range(0, LANES, members)], axis=0)
+    last = packed[height : height + 1]
+    cross, misfit, total = last[:, :members], last[:, members : members + 1], last[:, members + 1 : members + 2]
     rows = lax.broadcasted_iota(jnp.int32, (members, members), 0)
     cols = lax.broadcasted_iota(jnp.int32, (members, members), 1)
     eye = (rows == cols).astype(jnp.float32)
@@ -72,11 +81,44 @@
     return jnp.sqrt(dof) * zn / jnp.sqrt(scale) + wbar
 
 
+def cut(units, sizes):
+    out = []
+    while units:
+        out.insert(0, min(units, sizes[min(len(out), len(sizes) - 1)]))
+        units -= out[0]
+    return out
+
+
 def plan(piece):
     units = piece // UNIT
-    step = STEP if units % STEP == 0 else 1
-    late = max(1, round(units // step * LATE))
-    return units, step, units // step - late, late
+    late = max(1, round(units * LATE))
+    at, moves = 0, []
+    for part in cut(units - late, EARLY_SIZES), cut(late, LATE_SIZES):
+        moves.append([])
+        for n in part:
+            moves[-1].append((at, n))
+            at += n
+    return units, *moves
+
+
+def tiles(columns):
+    n = 1
+    while columns % (n * LANES) or columns // n > WIDE:
+        n += 1
+    return n, columns // n
+
+
+def mixing(tr):
+    members = tr.shape[0]
+    wt = tr.T.astype(jnp.bfloat16)
+    mean = jnp.full((16, members), 1.0 / members, jnp.bfloat16)
+    return jnp.concatenate([wt, mean], axis=0), 1.0 - jnp.sum(wt.astype(jnp.float32), axis=1, keepdims=True)
+
+
+def mix(lhs, coef, x):
+    members = x.shape[0]
+    mixed = jnp.dot(lhs, x, preferred_element_type=jnp.float32)
+    return (mixed[:members] + coef * mixed[members : members + 1]).astype(x.dtype)
 
 
 def sum_rounds(nmem, ncol):
@@ -102,8 +144,8 @@
     members = mk * nmem
     piece = sa.shape[1] // nmem
     nblk = idx.shape[2]
-    units, step, chunks, late_chunks = plan(piece)
-    early = chunks * step
+    units, early_moves, late_moves = plan(piece)
+    early = late_moves[0][0]
     late = units - early
     state, out = (sa, sb), (oa, ob)
     peers = [lax.rem(me + d, nmem) for d in range(1, nmem)]
@@ -158,28 +200,30 @@
         pl.semaphore_signal(barrier, inc=1, device_id=mate, device_id_type=MESH)
         pl.semaphore_wait(barrier, len(peers))
 
-    def move(slot, unit, size, g, d):
-        return pltpu.make_async_remote_copy(
-            state[g].at[:, cols_of(peers[d], unit, size)],
-            out[g].at[my_rows, pl.ds(pl.multiple_of(unit * UNIT, LANES), size * UNIT)],
-            st_s.at[slot],
-            st_r.at[slot],
-            device_id={"mem": peers[d]},
-            device_id_type=MESH,
-        )
-
     each = [(g, d) for g in range(2) for d in range(nmem - 1)]
-
-    def moves(q):
-        return [move(q * len(each) + n, q * step, step, g, d) for n, (g, d) in enumerate(each)]
-
-    def start(q, _):
-        for m in moves(q):
-            m.start()
-        return 0
-
-    first = min(FIRST, chunks)
-    start(0, 0)
+    moves = []
+    for at, size in early_moves + late_moves:
+        moves.append([])
+        for g, d in each:
+            slot = (len(moves) - 1) * len(each) + len(moves[-1])
+            moves[-1].append(
+                pltpu.make_async_remote_copy(
+                    state[g].at[:, cols_of(peers[d], at, size)],
+                    out[g].at[my_rows, pl.ds(at * UNIT, size * UNIT)],
+                    st_s.at[slot],
+                    st_r.at[slot],
+                    device_id={"mem": peers[d]},
+                    device_id_type=MESH,
+                )
+            )
+    first = len([at for at, _ in early_moves if 0 < at < FIRST]) + 1
+
+    def start(some):
+        for ms in some:
+            for m in ms:
+                m.start()
+
+    start(moves[:1])
     for c in loads + own:
         c.start()
 
@@ -212,7 +256,7 @@
             )
         )
         idx_copies[-1].start()
-    lax.fori_loop(1, first, start, 0)
+    start(moves[1:first])
 
     def gather(s, index):
         rows = s.shape[0]
@@ -262,7 +306,7 @@
         lax.fori_loop(0, late, own_row, 0)
     for c in hx_copies:
         c.start()
-    lax.fori_loop(first, chunks + late_chunks, start, 0)
+    start(moves[first:])
 
     def product(acc, x, value, weight):
         hmean = jnp.sum(x, axis=0, keepdims=True) / members
@@ -273,19 +317,20 @@
             preferred_element_type=jnp.float32,
         )
 
-    def early_sum(q, acc):
-        for m in moves(q):
-            m.wait_recv()
-        xs, vs, ws = [], [], []
-        for g in range(2):
-            for k in range(step):
-                u = q * step + k
-                xs.append(gather(out[g][:, unit_cols(u)], idx_f[g, pl.ds(u, 1), :]))
-                vs.append(val_f[g, pl.ds(u, 1), :])
-                ws.append(wgt_f[g, pl.ds(u, 1), :])
-        return product(acc, *(jnp.concatenate(t, axis=1) for t in (xs, vs, ws)))
-
-    acc = lax.fori_loop(0, chunks - 1, early_sum, jnp.zeros((ROWS, ROWS), jnp.float32))
+    def early_sum(u, acc):
+        for n, (at, _) in enumerate(early_moves):
+
+            @pl.when(u == at)
+            def _():
+                for m in moves[n]:
+                    m.wait_recv()
+
+        x = [gather(out[g][:, unit_cols(u)], idx_f[g, pl.ds(u, 1), :]) for g in range(2)]
+        value = [val_f[g, pl.ds(u, 1), :] for g in range(2)]
+        weight = [wgt_f[g, pl.ds(u, 1), :] for g in range(2)]
+        return product(acc, *(jnp.concatenate(t, axis=1) for t in (x, value, weight)))
+
+    acc = lax.fori_loop(0, early - 1, early_sum, jnp.zeros((ROWS, ROWS), jnp.float32))
     for c in hx_copies:
         c.wait()
 
@@ -300,14 +345,11 @@
         return product(acc, *(jnp.concatenate(t, axis=1) for t in (x, value, weight)))
 
     acc = lax.fori_loop(0, late, late_sum, acc)
-    acc = early_sum(chunks - 1, acc)
+    acc = early_sum(early - 1, acc)
 
     live = cnt[...].astype(jnp.float32)
     live = jnp.sum(jnp.sum(live, axis=1, keepdims=True), axis=0, keepdims=True)
-    used = res.shape[0]
-    rows = lax.broadcasted_iota(jnp.int32, (used, LANES), 0)
-    cols = lax.broadcasted_iota(jnp.int32, (used, LANES), 1)
-    acc = jnp.where((rows == members + 1) & (cols == members + 1), live, acc[:used])
+    acc = pack(acc, live, members)
 
     def to_mate(n, src, dst):
         return pltpu.make_async_remote_copy(
@@ -355,40 +397,23 @@
 
     weights = transform_of(res[...], members)
     tr[...] = weights
-    wt = weights.T.astype(jnp.bfloat16)
-    lhs[:members, :] = wt
-    lhs[members:, :] = jnp.full((16, members), 1.0 / members, jnp.bfloat16)
-    coef = 1.0 - jnp.sum(wt.astype(jnp.float32), axis=1, keepdims=True)
-
-    def mix(at, size):
-        where = pl.ds(pl.multiple_of(at, LANES), size)
+    left, coef = mixing(weights)
+    lhs[...] = left
+    count, width = tiles(early * UNIT)
+
+    def mix_tile(i, _):
+        where = pl.ds(pl.multiple_of(i * width, LANES), width)
         for g in range(2):
-            mixed = jnp.dot(lhs[...], out[g][:, where], preferred_element_type=jnp.float32)
-            xmean = mixed[members : members + 1]
-            out[g][:, where] = (mixed[:members] + coef * xmean).astype(jnp.bfloat16)
-
-    tile = TILE if (early * UNIT) % TILE == 0 else UNIT
-
-    def mix_early(i, _):
-        mix(i * tile, tile)
+            out[g][:, where] = mix(lhs[...], coef, out[g][:, where])
         return 0
 
-    lax.fori_loop(0, early * UNIT // tile, mix_early, 0)
-
-    def mix_late(q, _):
-        for m in moves(q):
+    lax.fori_loop(0, count, mix_tile, 0)
+    for ms in moves[len(early_moves) :]:
+        for m in ms:
             m.wait_recv()
-        mix(q * step * UNIT, step * UNIT)
-        return 0
-
-    lax.fori_loop(chunks, chunks + late_chunks, mix_late, 0)
-
-    def end(q, _):
-        for m in moves(q):
+    for ms in moves:
+        for m in ms:
             m.wait_send()
-        return 0
-
-    lax.fori_loop(0, chunks + late_chunks, end, 0)
 
     @pl.when(hub)
     def _():
@@ -401,12 +426,12 @@
     mk, held = state_a.shape
     piece = held // nmem
     members = mk * nmem
-    units, step, chunks, late_chunks = plan(piece)
-    late = late_chunks * step
+    units, early_moves, late_moves = plan(piece)
+    late = units - late_moves[0][0]
     rounds = sum_rounds(nmem, ncol)
     slots = 1 + sum(len(r) for r in rounds)
-    moves = 2 * (nmem - 1) * (chunks + late_chunks)
-    used = (members + 2 + 7) // 8 * 8
+    moves = 2 * (nmem - 1) * len(early_moves + late_moves)
+    used = members * members // LANES + 8
     dma = pltpu.SemaphoreType.DMA
     hbm = pl.BlockSpec(memory_space=pltpu.HBM)
     vmem = pl.BlockSpec(memory_space=pltpu.VMEM)
@@ -455,29 +480,46 @@
     )(*(pltpu.with_memory_space_constraint(x, pltpu.HBM) for x in (state_a, state_b, idx, val, wgt, cnt)))
 
 
-def write_kernel(parts, xa, xb, tr, oa, ob, ot, sems, tr_sem):
-    width = xa.shape[1] // parts
+def write_kernel(early, xa, xb, tr, oa, ob, ot, mixed, early_sem, late_sem, tr_sem):
     copies = [pltpu.make_async_copy(tr, ot, tr_sem)]
-    for i in range(parts):
+    count = early_sem.shape[1]
+    for i in range(count):
         for g, (x, o) in enumerate(((xa, oa), (xb, ob))):
-            where = pl.ds(i * width, width)
-            copies.append(pltpu.make_async_copy(x.at[:, where], o.at[:, where], sems.at[g, i]))
+            where = pl.ds(i * (early // count), early // count)
+            copies.append(pltpu.make_async_copy(x.at[:, where], o.at[:, where], early_sem.at[g, i]))
     for c in copies:
         c.start()
+    lhs, coef = mixing(tr[...])
+    width = mixed.shape[3]
+    for i in range(mixed.shape[0]):
+        for g, (x, o) in enumerate(((xa, oa), (xb, ob))):
+            where = pl.ds(early + i * width, width)
+            mixed[i, g] = mix(lhs, coef, x[:, where])
+            copies.append(pltpu.make_async_copy(mixed.at[i, g], o.at[:, where], late_sem.at[g, i]))
+            copies[-1].start()
     for c in copies:
         c.wait()
 
 
 def write(xa, xb, tr):
-    parts = 4
+    members, piece = xa.shape
+    early = plan(piece)[2][0][0] * UNIT
+    count, width = tiles(piece - early)
+    parts = 2
     vmem = pl.BlockSpec(memory_space=pltpu.VMEM)
     hbm = pl.BlockSpec(memory_space=pltpu.HBM)
+    dma = pltpu.SemaphoreType.DMA
     return pl.pallas_call(
-        functools.partial(write_kernel, parts),
+        functools.partial(write_kernel, early),
         out_shape=tuple(jax.ShapeDtypeStruct(x.shape, x.dtype) for x in (xa, xb, tr)),
         in_specs=[vmem, vmem, vmem],
         out_specs=(hbm, hbm, hbm),
-        scratch_shapes=[pltpu.SemaphoreType.DMA((2, parts)), pltpu.SemaphoreType.DMA],
+        scratch_shapes=[
+            pltpu.VMEM((count, 2, members, width), xa.dtype),
+            dma((2, parts)),
+            dma((2, count)),
+            dma,
+        ],
         compiler_params=pltpu.CompilerParams(vmem_limit_bytes=40 * 2**20),
         name="write",
     )(xa, xb, tr)

time: 104 us -> 103 us (level)
  no operation moved by 1% of the time
where the time goes in v3:
time: 103 us
  Pallas kernels  102 us (99%)
    pallas_call x1, Pallas kernels, exchange(): pl.pallas_call(functools.partial(exchange_kernel, nmem, ncol), out_shape=...  98.6 us
    pallas_call x1, Pallas kernels, write(): pl.pallas_call(functools.partial(write_kernel, early), out_shape=tuple((j...  3.38 us

profile of v3, /device:TPU:0, one launch (start us, length us, event | category | flops | bytes accessed | tf_op | source)
XLA Modules:
  0.0 102.7 jit_solution(10134631869738963977)
XLA Ops:
  0.6 98.6 %exchange.1 = (bf16[64,32768]{1,0:T(8,128)(2,1)S(1)}, bf16[64,32768]{1,0:T(8,128)(2,1)S(1)}, f32[64,64]{1,0:T(8,128)S(1)}) custom-call(bf16[32,65536]{1,0:T(8,128)(2,1)} %sa.1, bf16[32,65536]{1,0:T(8,128)(2,1)} %sb.1, s32[2,16,256]{2,1,0:T(8,128)} %bitcast.3, f32[2,16,256]{2,1,0:T(8,128)} %bitcast.4, f32[2,16,256]{2,1,0:T(8,128)} %bitcast.5, s32[2,256]{1,0:T(2,128)} %cnt_hbm.1), custom_call_target="tpu_custom_call" | custom-call | tf_op jit(solution)/shard_map/exchange/pallas_call | solution.py:438
  99.3 3.4 %write.1 = (bf16[64,32768]{1,0:T(8,128)(2,1)}, bf16[64,32768]{1,0:T(8,128)(2,1)}, f32[64,64]{1,0:T(8,128)}) custom-call(bf16[64,32768]{1,0:T(8,128)(2,1)S(1)} %get-tuple-element.6.xa, bf16[64,32768]{1,0:T(8,128)(2,1)S(1)} %get-tuple-element.7.xb, f32[64,64]{1,0:T(8,128)S(1)} %get-tuple-element.8.tr), custom_call_target="tpu_custom_call" | custom-call | tf_op jit(solution)/shard_map/write/pallas_call | solution.py:512

commit v4 on v3

--- a/solution.py
+++ b/solution.py
@@ -13,10 +13,11 @@
 MESH = pl.DeviceIdType.MESH
 ROWS = 128
 UNIT = 1024
-LATE = 0.3125
+LATE = 0.40625
 FIRST = 12
 EARLY_SIZES = (1, 2, 4)
 LATE_SIZES = (2, 4)
+REST = UNIT - LANES
 WIDE = 6144
 
 
@@ -135,7 +136,8 @@
 
 def exchange_kernel(
     nmem, ncol, sa, sb, idx_hbm, val_hbm, wgt_hbm, cnt_hbm, oa, ob, tr,
-    idx, val, wgt, cnt, table_sem, stage, idx_f, val_f, wgt_f, idx_tx, idx_in, tx, hx, cur, got, res, lhs,
+    idx, val, wgt, cnt, table_sem, stage, idx_f, val_f, wgt_f, idx_tx, idx_in,
+    from_s, from_c, at_s, back, tx, rest_tx, ahead_in, rest_in, hx, cur, got, res, lhs,
     own_sem, stage_sem, idx_s, idx_r, hx_s, hx_r, st_s, st_r, red_s, red_r, pair_s, pair_r, known,
 ):
     me = lax.axis_index("mem")
@@ -206,14 +208,16 @@
         moves.append([])
         for g, d in each:
             slot = (len(moves) - 1) * len(each) + len(moves[-1])
+            if at < early:
+                source = state[g].at[:, cols_of(peers[d], at, size)]
+                target = out[g].at[my_rows, pl.ds(at * UNIT, size * UNIT)]
+            else:
+                where = pl.ds((at - early) * REST, size * REST)
+                source, target = rest_tx.at[d, g, :, where], rest_in.at[me, g, :, where]
             moves[-1].append(
                 pltpu.make_async_remote_copy(
-                    state[g].at[:, cols_of(peers[d], at, size)],
-                    out[g].at[my_rows, pl.ds(at * UNIT, size * UNIT)],
-                    st_s.at[slot],
-                    st_r.at[slot],
-                    device_id={"mem": peers[d]},
-                    device_id_type=MESH,
+                    source, target, st_s.at[slot], st_r.at[slot],
+                    device_id={"mem": peers[d]}, device_id_type=MESH,
                 )
             )
     first = len([at for at, _ in early_moves if 0 < at < FIRST]) + 1
@@ -275,23 +279,90 @@
     def unit_cols(unit):
         return pl.ds(pl.multiple_of(unit * UNIT, LANES), UNIT)
 
+    def take(x, index):
+        return jnp.take_along_axis(x, jnp.broadcast_to(index, x.shape), axis=1)
+
+    shape = (late * 8, LANES)
+    lane = lax.broadcasted_iota(jnp.int32, shape, 1)
+    block = lax.rem(lax.broadcasted_iota(jnp.int32, shape, 0), 8)
+    lane_f = lane.astype(jnp.float32)
+    upto = (
+        lax.broadcasted_iota(jnp.int32, (LANES, LANES), 0)
+        <= lax.broadcasted_iota(jnp.int32, (LANES, LANES), 1)
+    ).astype(jnp.bfloat16)
+
+    def spread(rows):
+        return jnp.broadcast_to(rows[:, None, :], (late, 8, LANES)).reshape(shape)
+
+    def own_slots(x):
+        return jnp.sum(jnp.where(block == lane // 16, x, 0.0).reshape(late, 8, LANES), axis=1)
+
+    def ranks(table):
+        seen = jnp.zeros(shape, jnp.float32)
+        for s in range(16):
+            column = jnp.take_along_axis(table, block * 16 + s, axis=1)
+            seen = jnp.where(column == lane_f, 1.0, seen)
+        before = jnp.dot(seen.astype(jnp.bfloat16), upto, preferred_element_type=jnp.float32)
+        spare = 16.0 - before[:, LANES - 1 :]
+        other = lane_f + 1.0 - before
+        ahead = before + jnp.minimum(other, spare)
+        return (seen > 0.0) | (other <= spare), ahead, lane_f + 1.0 - ahead
+
+    def search(rank, limit):
+        at = jnp.zeros(shape, jnp.int32)
+        for b in (64, 32, 16, 8, 4, 2, 1):
+            here = jnp.take_along_axis(rank, at + (b - 1), axis=1)
+            at = jnp.where(here <= limit, at + b, at)
+        return at
+
+    for g in range(2):
+        table = spread(idx_tx[g].astype(jnp.float32))
+        goes, ahead, behind = ranks(table)
+        place = jnp.where(goes, (16 * block).astype(jnp.float32) + ahead - 1.0, LANES + behind - 1.0)
+        back[g] = place.astype(jnp.int32)
+        slots = own_slots(jnp.take_along_axis(ahead, table.astype(jnp.int32), axis=1))
+        first_lane = (lax.broadcasted_iota(jnp.int32, (late, LANES), 1) // 16) * 16
+        at_s[g] = slots.astype(jnp.int32) - 1 + first_lane
+
     for c in loads:
         c.wait()
+    for c in idx_copies:
+        c.wait()
+    tail = lax.broadcasted_iota(jnp.int32, (mk, LANES), 1) >= 112
+
+    def send_to(d, _):
+        for g in range(2):
+            table = spread(idx_in[nmem - 2 - d, g].astype(jnp.float32))
+            _, ahead, behind = ranks(table)
+            from_s[g] = own_slots(search(ahead, lax.rem(lane, 16).astype(jnp.float32)).astype(jnp.float32)).astype(jnp.int32)
+            source = search(behind, lane_f)
+            last = spread(source.astype(jnp.float32).reshape(late, 8, LANES)[:, 7, :])
+            last = jnp.take_along_axis(last, jnp.clip(16 * block + lane - 112, 0, LANES - 1), axis=1)
+            from_c[g] = jnp.where(lane < 112, source, last.astype(jnp.int32))
+
+        def send_row(u, _):
+            for g in range(2):
+                x = stage[d, g, :, unit_cols(u)].astype(jnp.float32)
+                tx[d, g, :, lanes_of(u)] = gather(x, from_s[g, pl.ds(u, 1), :]).astype(jnp.bfloat16)
+                rest = []
+                for t in range(7):
+                    index = from_c[g, pl.ds(u * 8 + t, 1), :]
+                    rest.append(
+                        jnp.where(tail, take(x[:, 7 * LANES :], index), take(x[:, t * LANES : (t + 1) * LANES], index))
+                    )
+                where = pl.ds(pl.multiple_of(u * REST, LANES), REST)
+                rest_tx[d, g, :, where] = jnp.concatenate(rest, axis=1).astype(jnp.bfloat16)
+            return 0
+
+        lax.fori_loop(0, late, send_row, 0)
+        return 0
+
+    lax.fori_loop(0, nmem - 1, send_to, 0)
     hx_copies = []
     for d, p in enumerate(peers):
-        src = nmem - 2 - d
-        idx_copies[src].wait()
-        for g in range(2):
-
-            def send_row(u, _):
-                picked = gather(stage[d, g, :, unit_cols(u)], idx_in[src, g, pl.ds(u, 1), :])
-                tx[d, g, :, lanes_of(u)] = picked.astype(jnp.bfloat16)
-                return 0
-
-            lax.fori_loop(0, late, send_row, 0)
         hx_copies.append(
             pltpu.make_async_remote_copy(
-                tx.at[d], hx.at[me], hx_s.at[d], hx_r.at[d], device_id={"mem": p}, device_id_type=MESH
+                tx.at[d], ahead_in.at[me], hx_s.at[d], hx_r.at[d], device_id={"mem": p}, device_id_type=MESH
             )
         )
     for c in own:
@@ -333,6 +404,16 @@
     acc = lax.fori_loop(0, early - 1, early_sum, jnp.zeros((ROWS, ROWS), jnp.float32))
     for c in hx_copies:
         c.wait()
+
+    def arrange(n, _):
+        p = lax.rem(me + 1 + n // late, nmem)
+        u = lax.rem(n, late)
+        for g in range(2):
+            x = ahead_in[p, g, :, lanes_of(u)].astype(jnp.float32)
+            hx[p, g, :, lanes_of(u)] = take(x, at_s[g, pl.ds(u, 1), :]).astype(jnp.bfloat16)
+        return 0
+
+    lax.fori_loop(0, (nmem - 1) * late, arrange, 0)
 
     def late_sum(u, acc):
         x, value, weight = [], [], []
@@ -408,9 +489,33 @@
         return 0
 
     lax.fori_loop(0, count, mix_tile, 0)
-    for ms in moves[len(early_moves) :]:
+    low = lax.broadcasted_iota(jnp.int32, (mk, LANES), 1)
+
+    def unpack(n, _):
+        p = lax.rem(me + 1 + lax.rem(n, nmem - 1), nmem)
+        u = n // (nmem - 1)
+        for g in range(2):
+            some = ahead_in[p, g, :, lanes_of(u)].astype(jnp.float32)
+            rest = rest_in[p, g, :, pl.ds(pl.multiple_of(u * REST, LANES), REST)].astype(jnp.float32)
+            rest = [rest[:, t * LANES : (t + 1) * LANES] for t in range(7)]
+            last = None
+            for t in range(7):
+                here = jnp.take_along_axis(rest[t], 112 + lax.rem(low, 16), axis=1)
+                last = here if last is None else jnp.where(low // 16 == t, here, last)
+            blocks = []
+            for t, other in enumerate(rest + [last]):
+                index = jnp.broadcast_to(back[g, pl.ds(u * 8 + t, 1), :], (mk, LANES))
+                inner = jnp.where(index < LANES, index, index - LANES)
+                blocks.append(jnp.where(index < LANES, take(some, inner), take(other, inner)))
+            rows = pl.ds(pl.multiple_of(p * mk, mk), mk)
+            out[g][rows, unit_cols(early + u)] = jnp.concatenate(blocks, axis=1).astype(jnp.bfloat16)
+        return 0
+
+    for (at, size), ms in zip(late_moves, moves[len(early_moves) :]):
         for m in ms:
             m.wait_recv()
+        begin = (at - early) * (nmem - 1)
+        lax.fori_loop(begin, begin + size * (nmem - 1), unpack, 0)
     for ms in moves:
         for m in ms:
             m.wait_send()
@@ -453,7 +558,14 @@
             pltpu.VMEM((2, units, LANES), jnp.float32),
             pltpu.VMEM((2, late, LANES), jnp.int32),
             pltpu.VMEM((nmem - 1, 2, late, LANES), jnp.int32),
+            pltpu.VMEM((2, late, LANES), jnp.int32),
+            pltpu.VMEM((2, late * 8, LANES), jnp.int32),
+            pltpu.VMEM((2, late, LANES), jnp.int32),
+            pltpu.VMEM((2, late * 8, LANES), jnp.int32),
             pltpu.VMEM((nmem - 1, 2, mk, late * LANES), jnp.bfloat16),
+            pltpu.VMEM((nmem - 1, 2, mk, late * REST), jnp.bfloat16),
+            pltpu.VMEM((nmem, 2, mk, late * LANES), jnp.bfloat16),
+            pltpu.VMEM((nmem, 2, mk, late * REST), jnp.bfloat16),
             pltpu.VMEM((nmem, 2, mk, late * LANES), jnp.bfloat16),
             pltpu.VMEM((max(1, len(rounds)), used, LANES), jnp.float32),
             pltpu.VMEM((slots, used, LANES), jnp.float32),

time: 103 us -> 99.9 us (0.970)
  Pallas kernels: 102 us -> 99.1 us
    pallas_call x1, Pallas kernels: 98.6 us -> 95.7 us  [exchange(): pl.pallas_call(functools.partial(exchange_kernel, nmem, ncol), out_shape=...]
where the time goes in v4:
time: 99.9 us; the launch traced here: 99.8 us
  Pallas kernels  99.1 us (99%)
    pallas_call x1, Pallas kernels, exchange(): pl.pallas_call(functools.partial(exchange_kernel, nmem, ncol), out_shape=...  95.7 us
    pallas_call x1, Pallas kernels, write(): pl.pallas_call(functools.partial(write_kernel, early), out_shape=tuple((j...  3.42 us

profile of v4, /device:TPU:0, one launch (start us, length us, event | category | flops | bytes accessed | tf_op | source)
XLA Modules:
  0.0 99.8 jit_solution(5396817259655265786)
XLA Ops:
  0.6 95.7 %exchange.1 = (bf16[64,32768]{1,0:T(8,128)(2,1)S(1)}, bf16[64,32768]{1,0:T(8,128)(2,1)S(1)}, f32[64,64]{1,0:T(8,128)S(1)}) custom-call(bf16[32,65536]{1,0:T(8,128)(2,1)} %sa.1, bf16[32,65536]{1,0:T(8,128)(2,1)} %sb.1, s32[2,16,256]{2,1,0:T(8,128)} %bitcast.3, f32[2,16,256]{2,1,0:T(8,128)} %bitcast.4, f32[2,16,256]{2,1,0:T(8,128)} %bitcast.5, s32[2,256]{1,0:T(2,128)} %cnt_hbm.1), custom_call_target="tpu_custom_call" | custom-call | tf_op jit(solution)/shard_map/exchange/pallas_call | solution.py:543
  96.4 3.4 %write.1 = (bf16[64,32768]{1,0:T(8,128)(2,1)}, bf16[64,32768]{1,0:T(8,128)(2,1)}, f32[64,64]{1,0:T(8,128)}) custom-call(bf16[64,32768]{1,0:T(8,128)(2,1)S(1)} %get-tuple-element.6.xa, bf16[64,32768]{1,0:T(8,128)(2,1)S(1)} %get-tuple-element.7.xb, f32[64,64]{1,0:T(8,128)S(1)} %get-tuple-element.8.tr), custom_call_target="tpu_custom_call" | custom-call | tf_op jit(solution)/shard_map/write/pallas_call | solution.py:624

commit v5 on v4

--- a/solution.py
+++ b/solution.py
@@ -13,10 +13,10 @@
 MESH = pl.DeviceIdType.MESH
 ROWS = 128
 UNIT = 1024
-LATE = 0.40625
-FIRST = 12
+LATE = 0.5
+FIRST = 16
 EARLY_SIZES = (1, 2, 4)
-LATE_SIZES = (2, 4)
+LATE_SIZES = (1, 2, 4)
 REST = UNIT - LANES
 WIDE = 6144
 
@@ -102,6 +102,10 @@
     return units, *moves
 
 
+def mixed_units(late_moves):
+    return late_moves[-2:][0][0]
+
+
 def tiles(columns):
     n = 1
     while columns % (n * LANES) or columns // n > WIDE:
@@ -124,18 +128,38 @@
 
 def sum_rounds(nmem, ncol):
     aside = 4 if ncol > 4 else 0
-    gens = [(b, aside) for b in bits(nmem)] + [(0, b) for b in bits(ncol) if b > 1]
-    rounds = []
+    rounds = [[(b, aside)] for b in bits(nmem)]
+    gens = [(0, b) for b in bits(ncol) if b > 1]
     for i in range(0, len(gens), 2):
         pair = gens[i : i + 2]
         if len(pair) == 2:
-            pair.append((pair[0][0] ^ pair[1][0], pair[0][1] ^ pair[1][1]))
+            pair.append((0, pair[0][1] ^ pair[1][1]))
         rounds.append(pair)
     return rounds
 
 
+def take(x, index):
+    return jnp.take_along_axis(x, jnp.broadcast_to(index, x.shape), axis=1)
+
+
+def unpack(some, rest, back):
+    some, rest = some.astype(jnp.float32), rest.astype(jnp.float32)
+    rest = [rest[:, t * LANES : (t + 1) * LANES] for t in range(7)]
+    lane = lax.broadcasted_iota(jnp.int32, some.shape, 1)
+    last = None
+    for t in range(7):
+        here = jnp.take_along_axis(rest[t], 112 + lax.rem(lane, 16), axis=1)
+        last = here if last is None else jnp.where(lane // 16 == t, here, last)
+    blocks = []
+    for t, other in enumerate(rest + [last]):
+        index = jnp.broadcast_to(back[t : t + 1], some.shape)
+        inner = jnp.where(index < LANES, index, index - LANES)
+        blocks.append(jnp.where(index < LANES, take(some, inner), take(other, inner)))
+    return jnp.concatenate(blocks, axis=1).astype(jnp.bfloat16)
+
+
 def exchange_kernel(
-    nmem, ncol, sa, sb, idx_hbm, val_hbm, wgt_hbm, cnt_hbm, oa, ob, tr,
+    nmem, ncol, sa, sb, idx_hbm, val_hbm, wgt_hbm, cnt_hbm, oa, ob, tr, some_out, rest_out, back_out,
     idx, val, wgt, cnt, table_sem, stage, idx_f, val_f, wgt_f, idx_tx, idx_in,
     from_s, from_c, at_s, back, tx, rest_tx, ahead_in, rest_in, hx, cur, got, res, lhs,
     own_sem, stage_sem, idx_s, idx_r, hx_s, hx_r, st_s, st_r, red_s, red_r, pair_s, pair_r, known,
@@ -214,6 +238,8 @@
             else:
                 where = pl.ds((at - early) * REST, size * REST)
                 source, target = rest_tx.at[d, g, :, where], rest_in.at[me, g, :, where]
+                if (at, size) == late_moves[-1]:
+                    target = rest_out.at[me, g]
             moves[-1].append(
                 pltpu.make_async_remote_copy(
                     source, target, st_s.at[slot], st_r.at[slot],
@@ -244,9 +270,9 @@
         return jnp.sum(jnp.where(diag[None], x, 0.0), axis=1)
 
     for g in range(2):
-        rows = flat(idx[g].astype(jnp.float32)).astype(jnp.int32)
-        idx_f[g] = rows
-        idx_tx[g] = rows[early:]
+        rows = flat(idx[g].astype(jnp.float32))
+        idx_f[g] = rows.astype(jnp.int32)
+        idx_tx[g] = rows[early:].astype(jnp.bfloat16)
     for g in range(2):
         live = slot_of < cnt[g : g + 1, :]
         wgt_f[g] = flat(jnp.where(live, wgt[g], 0.0))
@@ -279,9 +305,6 @@
     def unit_cols(unit):
         return pl.ds(pl.multiple_of(unit * UNIT, LANES), UNIT)
 
-    def take(x, index):
-        return jnp.take_along_axis(x, jnp.broadcast_to(index, x.shape), axis=1)
-
     shape = (late * 8, LANES)
     lane = lax.broadcasted_iota(jnp.int32, shape, 1)
     block = lax.rem(lax.broadcasted_iota(jnp.int32, shape, 0), 8)
@@ -320,6 +343,7 @@
         goes, ahead, behind = ranks(table)
         place = jnp.where(goes, (16 * block).astype(jnp.float32) + ahead - 1.0, LANES + behind - 1.0)
         back[g] = place.astype(jnp.int32)
+        back_out[g] = place[(late_moves[-1][0] - early) * 8 :].astype(jnp.int32)
         slots = own_slots(jnp.take_along_axis(ahead, table.astype(jnp.int32), axis=1))
         first_lane = (lax.broadcasted_iota(jnp.int32, (late, LANES), 1) // 16) * 16
         at_s[g] = slots.astype(jnp.int32) - 1 + first_lane
@@ -414,6 +438,7 @@
         return 0
 
     lax.fori_loop(0, (nmem - 1) * late, arrange, 0)
+    some_out[...] = ahead_in[:, :, :, (late_moves[-1][0] - early) * LANES :]
 
     def late_sum(u, acc):
         x, value, weight = [], [], []
@@ -489,33 +514,29 @@
         return 0
 
     lax.fori_loop(0, count, mix_tile, 0)
-    low = lax.broadcasted_iota(jnp.int32, (mk, LANES), 1)
-
-    def unpack(n, _):
+
+    def put_back(n, _):
         p = lax.rem(me + 1 + lax.rem(n, nmem - 1), nmem)
         u = n // (nmem - 1)
+        rows = pl.ds(pl.multiple_of(p * mk, mk), mk)
         for g in range(2):
-            some = ahead_in[p, g, :, lanes_of(u)].astype(jnp.float32)
-            rest = rest_in[p, g, :, pl.ds(pl.multiple_of(u * REST, LANES), REST)].astype(jnp.float32)
-            rest = [rest[:, t * LANES : (t + 1) * LANES] for t in range(7)]
-            last = None
-            for t in range(7):
-                here = jnp.take_along_axis(rest[t], 112 + lax.rem(low, 16), axis=1)
-                last = here if last is None else jnp.where(low // 16 == t, here, last)
-            blocks = []
-            for t, other in enumerate(rest + [last]):
-                index = jnp.broadcast_to(back[g, pl.ds(u * 8 + t, 1), :], (mk, LANES))
-                inner = jnp.where(index < LANES, index, index - LANES)
-                blocks.append(jnp.where(index < LANES, take(some, inner), take(other, inner)))
-            rows = pl.ds(pl.multiple_of(p * mk, mk), mk)
-            out[g][rows, unit_cols(early + u)] = jnp.concatenate(blocks, axis=1).astype(jnp.bfloat16)
+            out[g][rows, unit_cols(early + u)] = unpack(
+                ahead_in[p, g, :, lanes_of(u)],
+                rest_in[p, g, :, pl.ds(pl.multiple_of(u * REST, LANES), REST)],
+                back[g, pl.ds(pl.multiple_of(u * 8, 8), 8), :],
+            )
         return 0
 
     for (at, size), ms in zip(late_moves, moves[len(early_moves) :]):
         for m in ms:
             m.wait_recv()
-        begin = (at - early) * (nmem - 1)
-        lax.fori_loop(begin, begin + size * (nmem - 1), unpack, 0)
+        if (at, size) != late_moves[-1]:
+            begin = (at - early) * (nmem - 1)
+            lax.fori_loop(begin, begin + size * (nmem - 1), put_back, 0)
+        if at < mixed_units(late_moves):
+            where = pl.ds(at * UNIT, size * UNIT)
+            for g in range(2):
+                out[g][:, where] = mix(lhs[...], coef, out[g][:, where])
     for ms in moves:
         for m in ms:
             m.wait_send()
@@ -546,9 +567,12 @@
             pltpu.VMEM((members, piece), jnp.bfloat16),
             pltpu.VMEM((members, piece), jnp.bfloat16),
             pltpu.VMEM((members, members), jnp.float32),
+            pltpu.VMEM((nmem, 2, mk, late_moves[-1][1] * LANES), jnp.bfloat16),
+            pltpu.VMEM((nmem, 2, mk, late_moves[-1][1] * REST), jnp.bfloat16),
+            pltpu.VMEM((2, late_moves[-1][1] * 8, LANES), jnp.int32),
         ),
         in_specs=[hbm] * 6,
-        out_specs=(vmem, vmem, vmem),
+        out_specs=(vmem,) * 6,
         scratch_shapes=[
             *(pltpu.VMEM(x.shape, x.dtype) for x in (idx, val, wgt, cnt)),
             dma((4,)),
@@ -556,8 +580,8 @@
             pltpu.VMEM((2, units, LANES), jnp.int32),
             pltpu.VMEM((2, units, LANES), jnp.float32),
             pltpu.VMEM((2, units, LANES), jnp.float32),
-            pltpu.VMEM((2, late, LANES), jnp.int32),
-            pltpu.VMEM((nmem - 1, 2, late, LANES), jnp.int32),
+            pltpu.VMEM((2, late, LANES), jnp.bfloat16),
+            pltpu.VMEM((nmem - 1, 2, late, LANES), jnp.bfloat16),
             pltpu.VMEM((2, late, LANES), jnp.int32),
             pltpu.VMEM((2, late * 8, LANES), jnp.int32),
             pltpu.VMEM((2, late, LANES), jnp.int32),
@@ -592,49 +616,68 @@
     )(*(pltpu.with_memory_space_constraint(x, pltpu.HBM) for x in (state_a, state_b, idx, val, wgt, cnt)))
 
 
-def write_kernel(early, xa, xb, tr, oa, ob, ot, mixed, early_sem, late_sem, tr_sem):
+def write_kernel(nmem, ready, xa, xb, tr, some, rest, back, oa, ob, ot, mid, end, sems, tr_sem):
+    me = lax.axis_index("mem")
+    mk = xa.shape[0] // nmem
+    piece = xa.shape[1]
+    last = end.shape[2]
+    pairs = list(enumerate(((xa, oa), (xb, ob))))
     copies = [pltpu.make_async_copy(tr, ot, tr_sem)]
-    count = early_sem.shape[1]
-    for i in range(count):
-        for g, (x, o) in enumerate(((xa, oa), (xb, ob))):
-            where = pl.ds(i * (early // count), early // count)
-            copies.append(pltpu.make_async_copy(x.at[:, where], o.at[:, where], early_sem.at[g, i]))
+    half = ready // 2
+    for i in range(2):
+        for g, (x, o) in pairs:
+            where = pl.ds(i * half, half)
+            copies.append(pltpu.make_async_copy(x.at[:, where], o.at[:, where], sems.at[g, i]))
     for c in copies:
         c.start()
+
+    def send(g, n, source, target):
+        copies.append(pltpu.make_async_copy(source, target, sems.at[g, n]))
+        copies[-1].start()
+
     lhs, coef = mixing(tr[...])
-    width = mixed.shape[3]
-    for i in range(mixed.shape[0]):
-        for g, (x, o) in enumerate(((xa, oa), (xb, ob))):
-            where = pl.ds(early + i * width, width)
-            mixed[i, g] = mix(lhs, coef, x[:, where])
-            copies.append(pltpu.make_async_copy(mixed.at[i, g], o.at[:, where], late_sem.at[g, i]))
-            copies[-1].start()
+    if ready < piece - last:
+        for g, (x, o) in pairs:
+            where = pl.ds(ready, piece - last - ready)
+            mid[g] = mix(lhs, coef, x[:, where])
+            send(g, 2, mid.at[g], o.at[:, where])
+    for g, (x, o) in pairs:
+        where = pl.ds(piece - last, last)
+        end[g] = x[:, where]
+        for d in range(1, nmem):
+            p = lax.rem(me + d, nmem)
+            for u in range(last // UNIT):
+                end[g, pl.ds(pl.multiple_of(p * mk, mk), mk), u * UNIT : (u + 1) * UNIT] = unpack(
+                    some[p, g, :, u * LANES : (u + 1) * LANES],
+                    rest[p, g, :, u * REST : (u + 1) * REST],
+                    back[g, u * 8 : (u + 1) * 8, :],
+                )
+        end[g] = mix(lhs, coef, end[g])
+        send(g, 3, end.at[g], o.at[:, where])
     for c in copies:
         c.wait()
 
 
-def write(xa, xb, tr):
+def write(xa, xb, tr, some, rest, back):
     members, piece = xa.shape
-    early = plan(piece)[2][0][0] * UNIT
-    count, width = tiles(piece - early)
-    parts = 2
+    _, _, late_moves = plan(piece)
+    ready, last = mixed_units(late_moves) * UNIT, late_moves[-1][1] * UNIT
     vmem = pl.BlockSpec(memory_space=pltpu.VMEM)
     hbm = pl.BlockSpec(memory_space=pltpu.HBM)
-    dma = pltpu.SemaphoreType.DMA
     return pl.pallas_call(
-        functools.partial(write_kernel, early),
+        functools.partial(write_kernel, some.shape[0], ready),
         out_shape=tuple(jax.ShapeDtypeStruct(x.shape, x.dtype) for x in (xa, xb, tr)),
-        in_specs=[vmem, vmem, vmem],
+        in_specs=[vmem] * 6,
         out_specs=(hbm, hbm, hbm),
         scratch_shapes=[
-            pltpu.VMEM((count, 2, members, width), xa.dtype),
-            dma((2, parts)),
-            dma((2, count)),
-            dma,
+            pltpu.VMEM((2, members, max(LANES, piece - last - ready)), xa.dtype),
+            pltpu.VMEM((2, members, last), xa.dtype),
+            pltpu.SemaphoreType.DMA((2, 4)),
+            pltpu.SemaphoreType.DMA,
         ],
         compiler_params=pltpu.CompilerParams(vmem_limit_bytes=40 * 2**20),
         name="write",
-    )(xa, xb, tr)
+    )(xa, xb, tr, some, rest, back)
 
 
 def shards(state_a, state_b, obs_index, observation_count, obs_value, obs_weight):

time: 99.9 us -> 99.1 us (level)
  no operation moved by 1% of the time
where the time goes in v5:
time: 99.1 us; the launch traced here: 99 us
  Pallas kernels  98.3 us (99%)
    pallas_call x1, Pallas kernels, exchange(): pl.pallas_call(functools.partial(exchange_kernel, nmem, ncol), out_shape=...  94.9 us
    pallas_call x1, Pallas kernels, write(): pl.pallas_call(functools.partial(write_kernel, some.shape[0], ready), out...  3.41 us

profile of v5, /device:TPU:0, one launch (start us, length us, event | category | flops | bytes accessed | tf_op | source)
XLA Modules:
  0.0 99.0 jit_solution(4056581582705510896)
XLA Ops:
  0.6 94.9 %exchange.1 = (bf16[64,32768]{1,0:T(8,128)(2,1)S(1)}, bf16[64,32768]{1,0:T(8,128)(2,1)S(1)}, f32[64,64]{1,0:T(8,128)S(1)}, bf16[2,2,32,128]{3,2,1,0:T(8,128)(2,1...) custom-call(bf16[32,65536]{1,0:T(8,128)(2,1)} %sa.1, bf16[32,65536]{1,0:T(8,128)(2,1)} %sb.1, ...), custom_call_target="tpu_custom_call" | custom-call | tf_op jit(solution)/shard_map/exchange/pallas_call | solution.py:564
  95.6 3.4 %write.1 = (bf16[64,32768]{1,0:T(8,128)(2,1)}, bf16[64,32768]{1,0:T(8,128)(2,1)}, f32[64,64]{1,0:T(8,128)}) custom-call(bf16[64,32768]{1,0:T(8,128)(2,1)S(1)} %get-tuple-element.9.xa, bf16[64,32768]{1,0:T(8,128)(2,1)S(1)} %get-tuple-element.10.xb, f32[64,64]{1,0:T(8,128)S(1)} %get-tuple-element.11.tr, bf16[2,2,32,128]{3,2,1,0:T(8,128)(2,1)S(1)} %get-tuple-element.12.some, ...), custom_call_target="tpu_custom_call" | custom-call | tf_op jit(solution)/shard_map/write/pallas_call | solution.py:667

commit v6 on v5

--- a/solution.py
+++ b/solution.py
@@ -15,9 +15,10 @@
 UNIT = 1024
 LATE = 0.5
 FIRST = 16
-EARLY_SIZES = (1, 2, 4)
-LATE_SIZES = (1, 2, 4)
+EARLY_SIZES = (1, 3, 6)
+LATE_SIZES = (2, 4, 6)
 REST = UNIT - LANES
+PARTS = 4
 WIDE = 6144
 
 
@@ -207,12 +208,12 @@
     tables = []
     for n, (a, b) in enumerate(((idx_hbm, idx), (val_hbm, val), (wgt_hbm, wgt), (cnt_hbm, cnt))):
         tables.append(pltpu.make_async_copy(a, b, table_sem.at[n]))
-    for c in tables:
-        c.start()
 
     barrier = pltpu.get_barrier_semaphore()
     for p in peers:
         pl.semaphore_signal(barrier, inc=1, device_id={"mem": p}, device_id_type=MESH)
+    for c in tables:
+        c.start()
     @pl.when(hub)
     def _():
         for p in greeted:
@@ -623,8 +624,8 @@
     last = end.shape[2]
     pairs = list(enumerate(((xa, oa), (xb, ob))))
     copies = [pltpu.make_async_copy(tr, ot, tr_sem)]
-    half = ready // 2
-    for i in range(2):
+    half = ready // PARTS
+    for i in range(PARTS):
         for g, (x, o) in pairs:
             where = pl.ds(i * half, half)
             copies.append(pltpu.make_async_copy(x.at[:, where], o.at[:, where], sems.at[g, i]))
@@ -640,7 +641,7 @@
         for g, (x, o) in pairs:
             where = pl.ds(ready, piece - last - ready)
             mid[g] = mix(lhs, coef, x[:, where])
-            send(g, 2, mid.at[g], o.at[:, where])
+            send(g, PARTS, mid.at[g], o.at[:, where])
     for g, (x, o) in pairs:
         where = pl.ds(piece - last, last)
         end[g] = x[:, where]
@@ -653,7 +654,7 @@
                     back[g, u * 8 : (u + 1) * 8, :],
                 )
         end[g] = mix(lhs, coef, end[g])
-        send(g, 3, end.at[g], o.at[:, where])
+        send(g, PARTS + 1, end.at[g], o.at[:, where])
     for c in copies:
         c.wait()
 
@@ -672,7 +673,7 @@
         scratch_shapes=[
             pltpu.VMEM((2, members, max(LANES, piece - last - ready)), xa.dtype),
             pltpu.VMEM((2, members, last), xa.dtype),
-            pltpu.SemaphoreType.DMA((2, 4)),
+            pltpu.SemaphoreType.DMA((2, PARTS + 2)),
             pltpu.SemaphoreType.DMA,
         ],
         compiler_params=pltpu.CompilerParams(vmem_limit_bytes=40 * 2**20),

time: 99.1 us -> 99 us (level)
  no operation moved by 1% of the time
where the time goes in v6:
time: 99 us; the launch traced here: 98.8 us
  Pallas kernels  98.2 us (99%)
    pallas_call x1, Pallas kernels, exchange(): pl.pallas_call(functools.partial(exchange_kernel, nmem, ncol), out_shape=...  94.8 us
    pallas_call x1, Pallas kernels, write(): pl.pallas_call(functools.partial(write_kernel, some.shape[0], ready), out...  3.41 us

profile of v6, /device:TPU:0, one launch (start us, length us, event | category | flops | bytes accessed | tf_op | source)
XLA Modules:
  0.0 98.8 jit_solution(11882658354896181405)
XLA Ops:
  0.6 94.8 %exchange.1 = (bf16[64,32768]{1,0:T(8,128)(2,1)S(1)}, bf16[64,32768]{1,0:T(8,128)(2,1)S(1)}, f32[64,64]{1,0:T(8,128)S(1)}, bf16[2,2,32,256]{3,2,1,0:T(8,128)(2,1...) custom-call(bf16[32,65536]{1,0:T(8,128)(2,1)} %sa.1, bf16[32,65536]{1,0:T(8,128)(2,1)} %sb.1, ...), custom_call_target="tpu_custom_call" | custom-call | tf_op jit(solution)/shard_map/exchange/pallas_call | solution.py:565
  95.4 3.4 %write.1 = (bf16[64,32768]{1,0:T(8,128)(2,1)}, bf16[64,32768]{1,0:T(8,128)(2,1)}, f32[64,64]{1,0:T(8,128)}) custom-call(bf16[64,32768]{1,0:T(8,128)(2,1)S(1)} %get-tuple-element.9.xa, bf16[64,32768]{1,0:T(8,128)(2,1)S(1)} %get-tuple-element.10.xb, f32[64,64]{1,0:T(8,128)S(1)} %get-tuple-element.11.tr, bf16[2,2,32,256]{3,2,1,0:T(8,128)(2,1)S(1)} %get-tuple-element.12.some, ...), custom_call_target="tpu_custom_call" | custom-call | tf_op jit(solution)/shard_map/write/pallas_call | solution.py:668
